TPU v7x, 256 devices: a whole 4x4x8 slice. The times are simulated.
256 devices in a mesh: blk: 64 (over y_lo, z, x), mp: 4 (over y_hi, core).
Axes of the slice: x: 4, y: 4 (y_hi: 2, y_lo: 2; y = y_hi * 2 + y_lo), z: 8, core: 2. Of those that a mesh axis runs over, the one named last changes fastest.
Arguments:
- tokens: bfloat16 [64, 320, 7168], P('blk', 'mp'), may hold values from -6 to 6
- cotangent: bfloat16 [64, 320, 7168], P('blk', 'mp'), may hold values from -6 to 6
- gate_weight: bfloat16 [64, 7168, 512], P('blk', None, 'mp'), may hold values from -6 to 6
- up_weight: bfloat16 [64, 7168, 512], P('blk', None, 'mp'), may hold values from -6 to 6
- down_weight: bfloat16 [64, 512, 7168], P('blk', 'mp'), may hold values from -6 to 6
- mass: float32 [64], P('blk'), may hold values from 0.25 to 4
Outputs:
- gate_next: bfloat16 [64, 7168, 512], P('blk', None, 'mp')
- up_next: bfloat16 [64, 7168, 512], P('blk', None, 'mp')
- down_next: bfloat16 [64, 512, 7168], P('blk', 'mp')
- mass_next: float32 [64], P('blk')
- mass_total: float32 [], replicated
All inputs are finite; a program needn't handle non-finite values.
Results may differ from a plain program's by a relative error of at most 0.0051.
Values may be sent and summed in bfloat16 or wider, within the bound.
No kernel may reach another device: no remote copies, remote signals or barrier semaphores. Data moves between devices by JAX's collectives and lax.ppermute only.
A program may use at most 128 MiB of HBM per device.

v0:
```python
import jax
import jax.numpy as jnp
from jax import lax
from jax.sharding import PartitionSpec as P

step_size = 0.5


def sent_together(arrays, axis, dim, along):
    widths = [a.shape[along] for a in arrays]
    both = jnp.concatenate(arrays, axis=along)
    whole = lax.all_gather(both, axis, axis=dim, tiled=True)
    return tuple(jnp.split(whole, [sum(widths[:k]) for k in range(1, len(widths))], axis=along))


def passed_along(array, axis, by):
    count = lax.axis_size(axis)
    return lax.ppermute(array, axis, [(i, (i + by) % count) for i in range(count)])


def copy_for_each(array, axis):
    count = lax.axis_size(axis)
    return lax.all_to_all(
        jnp.broadcast_to(array[None], (count, *array.shape)), axis, 0, 0, tiled=True
    )


def of_everyone(array, axis):
    everything = copy_for_each(array, axis)
    return jnp.sum(everything, axis=0)


def on_device(tokens, cotangent, gate_weight, up_weight, down_weight, mass):
    whole_x, whole_dy = sent_together((tokens, cotangent), "mp", 1, 0)
    inputs = whole_x[0]
    grads_out = whole_dy[0]
    gate_w = gate_weight[0]
    up_w = up_weight[0]
    down_w = down_weight[0]
    width = gate_w.shape[0]
    units = gate_w.shape[1]
    inv_d = width ** (-0.5)
    inv_h = (units * lax.axis_size("mp")) ** (-0.5)
    coeffs = (3.0, 3.0, 1.0)
    summed_mass = mass
    moving_mass = mass
    for turn in range(3):
        moving_mass = passed_along(moving_mass, "blk", 1)
        summed_mass = summed_mass + coeffs[turn] * moving_mass
    mass_next = summed_mass / 8.0
    mass_total = of_everyone(jnp.sum(mass_next), "blk")
    gate_pre = jnp.dot(inputs, gate_w, preferred_element_type=jnp.float32) * inv_d
    up_pre = jnp.dot(inputs, up_w, preferred_element_type=jnp.float32) * inv_d
    sig = jax.nn.sigmoid(gate_pre)
    hidden = (gate_pre * sig * up_pre).astype(jnp.bfloat16)
    hidden_grad = (
        lax.dot_general(
            grads_out, down_w, (((1,), (1,)), ((), ())), preferred_element_type=jnp.float32
        )
        * inv_h
    )
    gate_gp = (hidden_grad * up_pre * sig * (1.0 + gate_pre * (1.0 - sig))).astype(jnp.bfloat16)
    up_gp = (hidden_grad * gate_pre * sig).astype(jnp.bfloat16)
    contract_rows = (((0,), (0,)), ((), ()))
    down_grad = (
        lax.dot_general(hidden, grads_out, contract_rows, preferred_element_type=jnp.float32)
        * inv_h
    )
    gate_grad = (
        lax.dot_general(inputs, gate_gp, contract_rows, preferred_element_type=jnp.float32) * inv_d
    )
    up_grad = (
        lax.dot_general(inputs, up_gp, contract_rows, preferred_element_type=jnp.float32) * inv_d
    )
    weight = mass[0]
    numer_gate = (weight * (gate_w.astype(jnp.float32) - step_size * gate_grad)).astype(
        jnp.bfloat16
    )
    numer_up = (weight * (up_w.astype(jnp.float32) - step_size * up_grad)).astype(jnp.bfloat16)
    numer_down = (weight * (down_w.astype(jnp.float32) - step_size * down_grad)).astype(
        jnp.bfloat16
    )
    stacked = jnp.stack([numer_gate, numer_up, numer_down.reshape(width, units)])
    summed = stacked.astype(jnp.float32)
    moving = stacked
    for turn in range(3):
        moving = passed_along(moving, "blk", 1)
        summed = summed + coeffs[turn] * moving.astype(jnp.float32)
    result = (summed / 8.0 / mass_next[0]).astype(jnp.bfloat16)
    gate_next = result[0][None]
    up_next = result[1][None]
    down_next = result[2].reshape(units, width)[None]
    return (gate_next, up_next, down_next, mass_next, mass_total)


def solution(mesh):
    in_specs = (
        P("blk", "mp", None),
        P("blk", "mp", None),
        P("blk", None, "mp"),
        P("blk", None, "mp"),
        P("blk", "mp", None),
        P("blk"),
    )
    out_specs = (P("blk", None, "mp"), P("blk", None, "mp"), P("blk", "mp", None), P("blk"), P())
    return jax.shard_map(
        on_device, mesh=mesh, in_specs=in_specs, out_specs=out_specs, check_vma=False
    )
```

profile of v0, /device:TPU:2, one launch (start us, length us, event | category | flops | bytes accessed | tf_op | source)
XLA Modules:
  0.0 536.8 jit_solution(16442934653239454286)
XLA Ops:
  7.2 3.3 pad_maximum_fusion.1
  11.2 71.8 %all-gather.2.cloned.1.call-done = bf16[2,320,7168]{2,1,0:T(8,128)(2,1)} async-done(((bf16[2,80,7168]{2,1,0:T(8,128)(2,1)}), bf16[2,320,7168]{2,1,0:T(8,128)(2,1)}) %all-gather.2.cloned.1.call-update) | async-done | bytes 9175056 | tf_op jit(solution)/shard_map/all_gather | solution.py:12
  83.0 3.8 fusion.20
  86.8 1.2 copy-done.3
  88.0 3.0 fusion.17
  91.0 2.6 fusion.8
  93.6 2.8 stack_reshape.3
  96.4 4.4 fusion.23
  100.8 4.8 fusion.10
  105.7 1.7 fusion.9
  107.9 0.8 copy-done.1
  108.7 1.5 collective-permute-start
  110.2 119.3 %collective-permute-done = bf16[3,7168,128]{2,1,0:T(8,128)(2,1)S(1)} collective-permute-done((bf16[3,7168,128]{2,1,0:T(8,128)(2,1)S(1)}, bf16[3,7168,128]{2,1,0:T(8,128)(2,1)S(1)}, u32[]{:S(2)}, u32[]{:S(2)}) %collective-permute-start) | collective-permute-done | bytes 5505056 | tf_op jit(solution)/shard_map/ppermute | solution.py:18
  229.5 2.4 copy-done.2
  231.9 1.5 collective-permute-start.1
  233.3 121.6 %collective-permute-done.1 = bf16[3,7168,128]{2,1,0:T(8,128)(2,1)} collective-permute-done((bf16[3,7168,128]{2,1,0:T(8,128)(2,1)S(1)}, bf16[3,7168,128]{2,1,0:T(8,128)(2,1)}, u32[]{:S(2)}, u32[]{:S(2)}) %collective-permute-start.1) | collective-permute-done | bytes 5505056 | tf_op jit(solution)/shard_map/ppermute | solution.py:18
  355.0 0.7 collective-permute-start.3
  355.6 123.0 %collective-permute-done.3 = f32[1]{0:T(128)} collective-permute-done((f32[1]{0:T(128)}, f32[1]{0:T(128)}, u32[]{:S(2)}, u32[]{:S(2)}) %collective-permute-start.3) | collective-permute-done | bytes 36 | tf_op jit(solution)/shard_map/ppermute | solution.py:18
  479.6 7.5 %collective-permute-done.4 = f32[1]{0:T(128)} collective-permute-done((f32[1]{0:T(128)}, f32[1]{0:T(128)}, u32[]{:S(2)}, u32[]{:S(2)}) %collective-permute-start.4) | collective-permute-done | bytes 36 | tf_op jit(solution)/shard_map/ppermute | solution.py:18
  487.8 7.8 %collective-permute-done.5 = f32[1]{0:T(128)} collective-permute-done((f32[1]{0:T(128)}, f32[1]{0:T(128)}, u32[]{:S(2)}, u32[]{:S(2)}) %collective-permute-start.5) | collective-permute-done | bytes 36 | tf_op jit(solution)/shard_map/ppermute | solution.py:18
  496.3 19.2 %all_to_all.6 = f32[64,1,1]{2,1,0:T(1,128)S(1)} all-to-all(f32[64,1,1]{2,1,0:T(1,128)S(1)} %broadcast_in_dim.2), channel_id=1, replica_groups=mesh['blk'=64,'mp'=4] {'blk'}, dimensions={0} | all-to-all | bytes 512 | tf_op jit(solution)/shard_map/all_to_all | solution.py:23
  516.2 8.8 %divide_convert_fusion = bf16[3,7168,128]{2,1,0:T(8,128)(2,1)S(1)} fusion(bf16[3,7168,128]{2,1,0:T(8,128)(2,1)} %collective-permute-done.2, bf16[3,7168,128]{2,1,0:T(8,128)(2,1)} %collective-permute-done.1, bf16[3,7168,128]{2,1,0:T(8,128)(2,1)} %copy-done.2, f32[]{:T(128)} %bitcast.8, bf16[1,7168,128]{2,1,0:T(8,128)(2,1)S(1)} %stack_reshape.3, ...), kind=kLoop, calls=%fused_computation | loop fusion | flops 38535168 | bytes 27525124 | tf_op jit(solution)/shard_map/convert_element_type | solution.py:89
  524.9 2.2 fusion.32
  527.1 1.7 broadcast_in_dim_reshape_squeeze.3
  (27 shorter events, 1.6 us)
Async XLA Ops:
  7.2 75.8 %copy-start.5 = (bf16[1,7168,128]{2,1,0:T(8,128)(2,1)S(1)}, bf16[1,7168,128]{2,1,0:T(8,128)(2,1)}, u32[]{:S(2)}) copy-start(bf16[1,7168,128]{2,1,0:T(8,128)(2,1)} %param.8) | copy-start | bytes 5505028
  7.2 75.8 %all-gather.2.cloned.1.call-start = ((), (), s32[]{:S(2)}) async-start(), calls=%async_computation.1 | async-start | bytes 11468800 | tf_op jit(solution)/shard_map/all_gather | solution.py:12
  83.0 5.0 copy-start.3
  88.0 3.0 copy-start.4
  96.4 9.2 %slice-start = ((s8[9175040]{0:T(1024)(128)(4,1)}), s8[4194304]{0:T(1024)(128)(4,1)S(1)}, s32[]{:S(2)}) async-start(s8[9175040]{0:T(1024)(128)(4,1)} %bitcast.43), calls=%async_computation.2 | async-start | bytes 8388608
  96.4 9.2 %slice-start.1 = ((s8[9175040]{0:T(1024)(128)(4,1)}), s8[4194304]{0:T(1024)(128)(4,1)S(1)}, s32[]{:S(2)}) async-start(s8[9175040]{0:T(1024)(128)(4,1)} %bitcast.43), calls=%async_computation.3 | async-start | bytes 8388608
  100.8 4.9 slice-start.2
  100.8 4.9 copy-start.6
  105.6 1.8 copy-start
  107.5 1.2 copy-start.1
  108.7 120.8 %collective-permute-start = (bf16[3,7168,128]{2,1,0:T(8,128)(2,1)S(1)}, bf16[3,7168,128]{2,1,0:T(8,128)(2,1)S(1)}, u32[]{:S(2)}, u32[]{:S(2)}) collective-permute-start(bf16[3,7168,128]{2,1,0:T(8,128)(2,1)S(1)} %pad_maximum_fusion), channel_id=1, source_target_pairs={{0,4},{4,8},{8,12},{12,16},{16,20},{20,24},{24,28},{28,32},{32,36}... | collective-permute-start | bytes 16515080 | tf_op jit(solution)/shard_map/ppermute | solution.py:18
  229.5 2.4 copy-start.2
  231.9 123.1 %collective-permute-start.1 = (bf16[3,7168,128]{2,1,0:T(8,128)(2,1)S(1)}, bf16[3,7168,128]{2,1,0:T(8,128)(2,1)}, u32[]{:S(2)}, u32[]{:S(2)}) collective-permute-start(bf16[3,7168,128]{2,1,0:T(8,128)(2,1)S(1)} %collective-permute-done), channel_id=1, source_target_pairs={{0,4},{4,8},{8,12},{12,16},{16,20},{20,24},{24,28},{28,32},{32,36}... | collective-permute-start | bytes 16515080 | tf_op jit(solution)/shard_map/ppermute | solution.py:18
  355.0 161.2 %collective-permute-start.2 = (bf16[3,7168,128]{2,1,0:T(8,128)(2,1)}, bf16[3,7168,128]{2,1,0:T(8,128)(2,1)}, u32[]{:S(2)}, u32[]{:S(2)}) collective-permute-start(bf16[3,7168,128]{2,1,0:T(8,128)(2,1)} %collective-permute-done.1), channel_id=1, source_target_pairs={{0,4},{4,8},{8,12},{12,16},{16,20},{20,24},{24,28},{28,32},{32,36}... | collective-permute-start | bytes 16515080 | tf_op jit(solution)/shard_map/ppermute | solution.py:18
  355.0 123.6 %collective-permute-start.3 = (f32[1]{0:T(128)}, f32[1]{0:T(128)}, u32[]{:S(2)}, u32[]{:S(2)}) collective-permute-start(f32[1]{0:T(128)} %param.11), channel_id=1, source_target_pairs={{0,4},{4,8},{8,12},{12,16},{16,20},{20,24},{24,28},{28,32},{32,36}... | collective-permute-start | bytes 20 | tf_op jit(solution)/shard_map/ppermute | solution.py:18
  479.3 7.8 %collective-permute-start.4 = (f32[1]{0:T(128)}, f32[1]{0:T(128)}, u32[]{:S(2)}, u32[]{:S(2)}) collective-permute-start(f32[1]{0:T(128)} %collective-permute-done.3), channel_id=1, source_target_pairs={{0,4},{4,8},{8,12},{12,16},{16,20},{20,24},{24,28},{28,32},{32,36}... | collective-permute-start | bytes 20 | tf_op jit(solution)/shard_map/ppermute | solution.py:18
  487.7 7.9 %collective-permute-start.5 = (f32[1]{0:T(128)}, f32[1]{0:T(128)}, u32[]{:S(2)}, u32[]{:S(2)}) collective-permute-start(f32[1]{0:T(128)} %collective-permute-done.4), channel_id=1, source_target_pairs={{0,4},{4,8},{8,12},{12,16},{16,20},{20,24},{24,28},{28,32},{32,36}... | collective-permute-start | bytes 20 | tf_op jit(solution)/shard_map/ppermute | solution.py:18
Sparse Core Ops, SparseCore 0:
  10.7 72.2 all-gather.1
where the time goes:
time: 537 us
  waiting for transfers between devices  451 us (84%)
  matrix products  20.3 us (4%)
  blocking collectives  19.2 us (4%)
  between operations  18 us (3%)
  other arithmetic  13.2 us (2%)
  local copies, waits for them, and re-layouts  11 us (2%)
    ppermute x6, waiting for transfers between devices, passed_along(): lax.ppermute(array, axis, [(i, (i + by) % count) for i in range(count)])  379 us
    all_gather x1, waiting for transfers between devices, sent_together(): whole = lax.all_gather(both, axis, axis=dim, tiled=True)  71.8 us
    all_to_all x1, blocking collectives, copy_for_each(): lax.all_to_all(jnp.broadcast_to(array[None], (count, *array.shape)), axis...  19.2 us
  transfers between devices with their start and end apart: 7, of which 6 were waited for; matrix products, arithmetic and copies ran while one was open for 0% of the time, Pallas kernels for 0%

commit v1 on v0

v1 whole, which is shorter than its diff:
```python
import jax
import jax.numpy as jnp
from jax import lax
from jax.sharding import PartitionSpec as P


step_size = 0.5
ROW = 4
DOWN_CUTS = (0, 18, 37, 56)
GATE_CUTS = (0, 19, 38, 56)
UP_CUTS = (0, 19, 38, 56)


def cuts(width, marks):
    return [slice(width * a // 56, width * b // 56) for a, b in zip(marks[:-1], marks[1:])]


def swapped(array, mask):
    count = lax.axis_size("mp")
    return lax.ppermute(array, "mp", [(i, i ^ mask) for i in range(count)])


def moved(array, shift):
    count = lax.axis_size("blk")
    pairs = [(r, (r + shift[r % ROW]) % count) for r in range(count) if shift[r % ROW] is not None]
    return lax.ppermute(array, "blk", pairs)


def everyone(value):
    count = lax.axis_size("blk")
    ring = jnp.where(lax.iota(jnp.int32, count) == lax.axis_index("blk"), value, 0.0)
    bits = [1 << k for k in range(count.bit_length() - 1)]
    for bit in bits:
        other = lax.ppermute(ring, "blk", [(r, r ^ bit) for r in range(count)])
        ring = ring + other
    return ring


def mixed(numer, place, scale):
    f32 = jnp.float32
    even = place % 2 == 0
    above = moved(numer, (None, 4, 4, 4))
    crossing = jnp.where(place < 2, numer, above)
    got = moved(crossing, (3, 1, -1, -3))
    part = jnp.where(even, 3.0 * numer.astype(f32), above.astype(f32)) + 3.0 * got.astype(f32)
    part = part.astype(jnp.bfloat16)
    partner = moved(part, (1, -1, 1, -1))
    total = numer.astype(f32) + jnp.where(even, 3.0, 1.0) * got.astype(f32)
    return ((total + partner.astype(f32)) * scale).astype(jnp.bfloat16)


def on_device(tokens, cotangent, gate_weight, up_weight, down_weight, mass):
    f32 = jnp.float32
    bf16 = jnp.bfloat16
    x0 = tokens[0]
    d0 = cotangent[0]
    gate_w = gate_weight[0]
    up_w = up_weight[0]
    down_w = down_weight[0]
    width = gate_w.shape[0]
    units = gate_w.shape[1]
    inv_d = width ** (-0.5)
    inv_h = (units * lax.axis_size("mp")) ** (-0.5)
    spans = cuts(width, DOWN_CUTS)
    gate_spans = cuts(width, GATE_CUTS)
    up_spans = cuts(width, UP_CUTS)

    x2 = swapped(x0, 2)
    x1 = swapped(x0, 1)
    d2 = [swapped(d0[:, s], 2) for s in spans]
    d1 = swapped(d0, 1)
    x3 = swapped(x2, 1)
    d3 = [swapped(d, 1) for d in d2]

    me = lax.axis_index("blk")
    masses = everyone(mass)
    next_all = (
        masses + 3.0 * jnp.roll(masses, 1) + 3.0 * jnp.roll(masses, 2) + jnp.roll(masses, 3)
    ) / 8.0
    mass_total = jnp.sum(next_all)
    mass_next = lax.dynamic_slice(next_all, (me,), (1,))
    place = me % ROW
    scale = 0.125 / mass_next[0]

    x = jnp.concatenate([x0, x1, x2, x3], axis=0)
    gate_pre = jnp.dot(x, gate_w, preferred_element_type=f32) * inv_d
    up_pre = jnp.dot(x, up_w, preferred_element_type=f32) * inv_d
    sig = jax.nn.sigmoid(gate_pre)
    hidden = (gate_pre * sig * up_pre).astype(bf16)

    dy = [jnp.concatenate([d0[:, s], d1[:, s], d2[c], d3[c]], axis=0) for c, s in enumerate(spans)]
    weight = mass[0]
    rows = (((0,), (0,)), ((), ()))

    def numer(w, lhs, rhs, scale_by):
        grad = lax.dot_general(lhs, rhs, rows, preferred_element_type=f32) * scale_by
        return (weight * (w.astype(f32) - step_size * grad)).astype(bf16)

    down_numer = [numer(down_w[:, s], hidden, dy[c], inv_h) for c, s in enumerate(spans)]
    down_next = [mixed(n, place, scale) for n in down_numer]
    gate_pre, up_pre, _ = lax.optimization_barrier((gate_pre, up_pre, down_numer[-1]))
    sig = jax.nn.sigmoid(gate_pre)
    hidden_grad = 0.0
    for c, s in enumerate(spans):
        hidden_grad = hidden_grad + lax.dot_general(
            dy[c], down_w[:, s], (((1,), (1,)), ((), ())), preferred_element_type=f32
        )
    hidden_grad = hidden_grad * inv_h
    gate_gp = (hidden_grad * up_pre * sig * (1.0 + gate_pre * (1.0 - sig))).astype(bf16)
    up_gp = (hidden_grad * gate_pre * sig).astype(bf16)
    gate_next = [mixed(numer(gate_w[s], x[:, s], gate_gp, inv_d), place, scale) for s in gate_spans]
    up_next = [mixed(numer(up_w[s], x[:, s], up_gp, inv_d), place, scale) for s in up_spans]
    return (
        jnp.concatenate(gate_next, axis=0)[None],
        jnp.concatenate(up_next, axis=0)[None],
        jnp.concatenate(down_next, axis=1)[None],
        mass_next,
        mass_total,
    )


def solution(mesh):
    in_specs = (
        P("blk", "mp", None),
        P("blk", "mp", None),
        P("blk", None, "mp"),
        P("blk", None, "mp"),
        P("blk", "mp", None),
        P("blk"),
    )
    out_specs = (P("blk", None, "mp"), P("blk", None, "mp"), P("blk", "mp", None), P("blk"), P())

    return jax.shard_map(
        on_device, mesh=mesh, in_specs=in_specs, out_specs=out_specs, check_vma=False
    )
```

time: 537 us -> 376 us (0.70)
  the two profiles are of different devices: /device:TPU:2 before, /device:TPU:6 now
where the time goes in v1:
time: 376 us; the launch traced here: 368 us
  waiting for transfers between devices  262 us (70%)
  starting transfers between devices  67.7 us (18%)
  matrix products  17.1 us (5%)
  other arithmetic  12.2 us (3%)
  local copies, waits for them, and re-layouts  6.45 us (2%)
    ppermute x27, waiting for transfers between devices, moved(): return lax.ppermute(array, 'blk', pairs)  234 us
    ppermute x27, starting transfers between devices, moved(): return lax.ppermute(array, 'blk', pairs)  42.1 us
    ppermute x6, waiting for transfers between devices, everyone(): other = lax.ppermute(ring, 'blk', [(r, r ^ bit) for r in range(count)])  20.3 us
    ppermute x6, starting transfers between devices, everyone(): other = lax.ppermute(ring, 'blk', [(r, r ^ bit) for r in range(count)])  15.5 us
    ppermute x10, starting transfers between devices, swapped(): return lax.ppermute(array, 'mp', [(i, i ^ mask) for i in range(count)])  10.1 us
    dot_general x9, matrix products, numer(): lax.dot_general(lhs, rhs, rows, preferred_element_type=f32) * scale_by  9.3 us
    ppermute x10, waiting for transfers between devices, swapped(): return lax.ppermute(array, 'mp', [(i, i ^ mask) for i in range(count)])  8.17 us
  transfers between devices with their start and end apart: 43, of which 23 were waited for; matrix products, arithmetic and copies ran while one was open for 9% of the time, Pallas kernels for 0%

profile of v1, /device:TPU:6, one launch (start us, length us, event | category | flops | bytes accessed | tf_op | source)
XLA Modules:
  0.0 368.5 jit_solution(14090148442859321860)
XLA Ops:
  20.8 6.8 %collective-permute-start.17 = (f32[64]{0:T(128)S(1)}, f32[64]{0:T(128)S(1)}, u32[]{:S(2)}, u32[]{:S(2)}) collective-permute-start(f32[64]{0:T(128)S(1)} %add.154), channel_id=1, source_target_pairs={{0,64},{4,68},{8,72},{12,76},{16,80},{20,84},{24,88},{28,92},{32,9... | collective-permute-start | bytes 776 | tf_op jit(solution)/shard_map/ppermute | solution.py:34
  32.2 15.5 %collective-permute-done.18 = f32[64]{0:T(128)S(1)} collective-permute-done((f32[64]{0:T(128)S(1)}, f32[64]{0:T(128)S(1)}, u32[]{:S(2)}, u32[]{:S(2)}) %collective-permute-start.18) | collective-permute-done | bytes 288 | tf_op jit(solution)/shard_map/ppermute | solution.py:34
  53.0 5.9 %collective-permute-done.4 = bf16[80,2304]{1,0:T(8,128)(2,1)} collective-permute-done((bf16[80,2304]{1,0:T(8,128)(2,1)}, bf16[80,2304]{1,0:T(8,128)(2,1)}, u32[]{:S(2)}, u32[]{:S(2)}) %collective-permute-start.4) | collective-permute-done | bytes 368672 | tf_op jit(solution)/shard_map/ppermute | solution.py:20
  72.3 3.8 %collective-permute-start.40 = (bf16[128,2432]{1,0:T(8,128)(2,1)S(1)}, bf16[128,2432]{1,0:T(8,128)(2,1)S(1)}, u32[]{:S(2)}, u32[]{:S(2)}) collective-permute-start(bf16[128,2432]{1,0:T(8,128)(2,1)S(1)} %fusion.21), channel_id=1, source_target_pairs={{4,20},{8,24},{12,28},{20,36},{24,40},{28,44},{36,52},{40,56},{44,... | collective-permute-start | bytes 1867784 | tf_op jit(solution)/shard_map/ppermute | solution.py:26
  78.6 3.8 %collective-permute-start.22 = (bf16[2304,128]{1,0:T(8,128)(2,1)S(1)}, bf16[2304,128]{1,0:T(8,128)(2,1)S(1)}, u32[]{:S(2)}, u32[]{:S(2)}) collective-permute-start(bf16[2304,128]{1,0:T(8,128)(2,1)S(1)} %fusion.18), channel_id=1, source_target_pairs={{4,20},{8,24},{12,28},{20,36},{24,40},{28,44},{36,52},{40,56},{44,... | collective-permute-start | bytes 1769480 | tf_op jit(solution)/shard_map/ppermute | solution.py:26
  83.2 3.8 %collective-permute-start.19 = (bf16[2432,128]{1,0:T(8,128)(2,1)S(1)}, bf16[2432,128]{1,0:T(8,128)(2,1)S(1)}, u32[]{:S(2)}, u32[]{:S(2)}) collective-permute-start(bf16[2432,128]{1,0:T(8,128)(2,1)S(1)} %fusion.23), channel_id=1, source_target_pairs={{4,20},{8,24},{12,28},{20,36},{24,40},{28,44},{36,52},{40,56},{44,... | collective-permute-start | bytes 1867784 | tf_op jit(solution)/shard_map/ppermute | solution.py:26
  87.8 5.0 %collective-permute-start.10 = (bf16[2432,128]{1,0:T(8,128)(2,1)S(1)}, bf16[2432,128]{1,0:T(8,128)(2,1)S(1)}, u32[]{:S(2)}, u32[]{:S(2)}) collective-permute-start(bf16[2432,128]{1,0:T(8,128)(2,1)S(1)} %fusion.22), channel_id=1, source_target_pairs={{4,20},{8,24},{12,28},{20,36},{24,40},{28,44},{36,52},{40,56},{44,... | collective-permute-start | bytes 1867784 | tf_op jit(solution)/shard_map/ppermute | solution.py:26
  101.2 7.1 %collective-permute-done.22 = bf16[2304,128]{1,0:T(8,128)(2,1)S(1)} collective-permute-done((bf16[2304,128]{1,0:T(8,128)(2,1)S(1)}, bf16[2304,128]{1,0:T(8,128)(2,1)S(1)}, u32[]{:S(2)}, u32[]{:S(2)}) %collective-permute-start.22) | collective-permute-done | bytes 589856 | tf_op jit(solution)/shard_map/ppermute | solution.py:26
  110.3 37.3 %collective-permute-done.31 = bf16[2304,128]{1,0:T(8,128)(2,1)S(1)} collective-permute-done((bf16[2304,128]{1,0:T(8,128)(2,1)S(1)}, bf16[2304,128]{1,0:T(8,128)(2,1)S(1)}, u32[]{:S(2)}, u32[]{:S(2)}) %collective-permute-start.31) | collective-permute-done | bytes 589856 | tf_op jit(solution)/shard_map/ppermute | solution.py:26
  149.7 23.4 %collective-permute-done.34 = bf16[128,2304]{1,0:T(8,128)(2,1)S(1)} collective-permute-done((bf16[128,2304]{1,0:T(8,128)(2,1)S(1)}, bf16[128,2304]{1,0:T(8,128)(2,1)S(1)}, u32[]{:S(2)}, u32[]{:S(2)}) %collective-permute-start.34) | collective-permute-done | bytes 589856 | tf_op jit(solution)/shard_map/ppermute | solution.py:26
  180.9 13.1 %collective-permute-done.25 = bf16[2432,128]{1,0:T(8,128)(2,1)S(1)} collective-permute-done((bf16[2432,128]{1,0:T(8,128)(2,1)S(1)}, bf16[2432,128]{1,0:T(8,128)(2,1)S(1)}, u32[]{:S(2)}, u32[]{:S(2)}) %collective-permute-start.25) | collective-permute-done | bytes 622624 | tf_op jit(solution)/shard_map/ppermute | solution.py:26
  197.5 8.5 %collective-permute-done.37 = bf16[128,2432]{1,0:T(8,128)(2,1)S(1)} collective-permute-done((bf16[128,2432]{1,0:T(8,128)(2,1)S(1)}, bf16[128,2432]{1,0:T(8,128)(2,1)S(1)}, u32[]{:S(2)}, u32[]{:S(2)}) %collective-permute-start.37) | collective-permute-done | bytes 622624 | tf_op jit(solution)/shard_map/ppermute | solution.py:26
  210.1 9.8 %collective-permute-done.35 = bf16[128,2304]{1,0:T(8,128)(2,1)S(1)} collective-permute-done((bf16[128,2304]{1,0:T(8,128)(2,1)S(1)}, bf16[128,2304]{1,0:T(8,128)(2,1)S(1)}, u32[]{:S(2)}, u32[]{:S(2)}) %collective-permute-start.35) | collective-permute-done | bytes 589856 | tf_op jit(solution)/shard_map/ppermute | solution.py:26
  220.2 13.0 %collective-permute-done.20 = bf16[2432,128]{1,0:T(8,128)(2,1)S(1)} collective-permute-done((bf16[2432,128]{1,0:T(8,128)(2,1)S(1)}, bf16[2432,128]{1,0:T(8,128)(2,1)S(1)}, u32[]{:S(2)}, u32[]{:S(2)}) %collective-permute-start.20) | collective-permute-done | bytes 622624 | tf_op jit(solution)/shard_map/ppermute | solution.py:26
  233.6 13.0 %collective-permute-done.11 = bf16[2432,128]{1,0:T(8,128)(2,1)S(1)} collective-permute-done((bf16[2432,128]{1,0:T(8,128)(2,1)S(1)}, bf16[2432,128]{1,0:T(8,128)(2,1)S(1)}, u32[]{:S(2)}, u32[]{:S(2)}) %collective-permute-start.11) | collective-permute-done | bytes 622624 | tf_op jit(solution)/shard_map/ppermute | solution.py:26
  246.9 13.0 %collective-permute-done.29 = bf16[2432,128]{1,0:T(8,128)(2,1)S(1)} collective-permute-done((bf16[2432,128]{1,0:T(8,128)(2,1)S(1)}, bf16[2432,128]{1,0:T(8,128)(2,1)S(1)}, u32[]{:S(2)}, u32[]{:S(2)}) %collective-permute-start.29) | collective-permute-done | bytes 622624 | tf_op jit(solution)/shard_map/ppermute | solution.py:26
  260.3 13.0 %collective-permute-done.26 = bf16[2432,128]{1,0:T(8,128)(2,1)S(1)} collective-permute-done((bf16[2432,128]{1,0:T(8,128)(2,1)S(1)}, bf16[2432,128]{1,0:T(8,128)(2,1)S(1)}, u32[]{:S(2)}, u32[]{:S(2)}) %collective-permute-start.26) | collective-permute-done | bytes 622624 | tf_op jit(solution)/shard_map/ppermute | solution.py:26
  273.6 13.0 %collective-permute-done.41 = bf16[128,2432]{1,0:T(8,128)(2,1)S(1)} collective-permute-done((bf16[128,2432]{1,0:T(8,128)(2,1)S(1)}, bf16[128,2432]{1,0:T(8,128)(2,1)S(1)}, u32[]{:S(2)}, u32[]{:S(2)}) %collective-permute-start.41) | collective-permute-done | bytes 622624 | tf_op jit(solution)/shard_map/ppermute | solution.py:26
  286.9 11.6 %collective-permute-done.38 = bf16[128,2432]{1,0:T(8,128)(2,1)S(1)} collective-permute-done((bf16[128,2432]{1,0:T(8,128)(2,1)S(1)}, bf16[128,2432]{1,0:T(8,128)(2,1)S(1)}, u32[]{:S(2)}, u32[]{:S(2)}) %collective-permute-start.38) | collective-permute-done | bytes 622624 | tf_op jit(solution)/shard_map/ppermute | solution.py:26
  304.8 10.7 %collective-permute-done.12 = bf16[2432,128]{1,0:T(8,128)(2,1)S(1)} collective-permute-done((bf16[2432,128]{1,0:T(8,128)(2,1)S(1)}, bf16[2432,128]{1,0:T(8,128)(2,1)S(1)}, u32[]{:S(2)}, u32[]{:S(2)}) %collective-permute-start.12) | collective-permute-done | bytes 622624 | tf_op jit(solution)/shard_map/ppermute | solution.py:26
  317.1 11.7 %collective-permute-done.30 = bf16[2432,128]{1,0:T(8,128)(2,1)S(1)} collective-permute-done((bf16[2432,128]{1,0:T(8,128)(2,1)S(1)}, bf16[2432,128]{1,0:T(8,128)(2,1)S(1)}, u32[]{:S(2)}, u32[]{:S(2)}) %collective-permute-start.30) | collective-permute-done | bytes 622624 | tf_op jit(solution)/shard_map/ppermute | solution.py:26
  329.1 13.0 %collective-permute-done.27 = bf16[2432,128]{1,0:T(8,128)(2,1)S(1)} collective-permute-done((bf16[2432,128]{1,0:T(8,128)(2,1)S(1)}, bf16[2432,128]{1,0:T(8,128)(2,1)S(1)}, u32[]{:S(2)}, u32[]{:S(2)}) %collective-permute-start.27) | collective-permute-done | bytes 622624 | tf_op jit(solution)/shard_map/ppermute | solution.py:26
  343.8 11.7 %collective-permute-done.42 = bf16[128,2432]{1,0:T(8,128)(2,1)S(1)} collective-permute-done((bf16[128,2432]{1,0:T(8,128)(2,1)S(1)}, bf16[128,2432]{1,0:T(8,128)(2,1)S(1)}, u32[]{:S(2)}, u32[]{:S(2)}) %collective-permute-start.42) | collective-permute-done | bytes 622624 | tf_op jit(solution)/shard_map/ppermute | solution.py:26
  355.8 10.8 %collective-permute-done.39 = bf16[128,2432]{1,0:T(8,128)(2,1)S(1)} collective-permute-done((bf16[128,2432]{1,0:T(8,128)(2,1)S(1)}, bf16[128,2432]{1,0:T(8,128)(2,1)S(1)}, u32[]{:S(2)}, u32[]{:S(2)}) %collective-permute-start.39) | collective-permute-done | bytes 622624 | tf_op jit(solution)/shard_map/ppermute | solution.py:26
  (132 shorter events, 87.1 us)
Async XLA Ops:
  2.3 57.2 %collective-permute-start.1 = (bf16[80,7168]{1,0:T(8,128)(2,1)}, bf16[80,7168]{1,0:T(8,128)(2,1)S(1)}, u32[]{:S(2)}, u32[]{:S(2)}) collective-permute-start(bf16[80,7168]{1,0:T(8,128)(2,1)} %bitcast.69), channel_id=1, source_target_pairs={{0,2},{1,3},{2,0},{3,1},{4,6},{5,7},{6,4},{7,5},{8,10},{9,11},{10,... | collective-permute-start | bytes 3440648 | tf_op jit(solution)/shard_map/ppermute | solution.py:20
  5.5 54.4 %collective-permute-start.3 = (bf16[80,7168]{1,0:T(8,128)(2,1)}, bf16[80,7168]{1,0:T(8,128)(2,1)S(1)}, u32[]{:S(2)}, u32[]{:S(2)}) collective-permute-start(bf16[80,7168]{1,0:T(8,128)(2,1)} %bitcast.73), channel_id=1, source_target_pairs={{0,1},{1,0},{2,3},{3,2},{4,5},{5,4},{6,7},{7,6},{8,9},{9,8},{10,11... | collective-permute-start | bytes 3440648 | tf_op jit(solution)/shard_map/ppermute | solution.py:20
  8.8 50.2 %collective-permute-start.8 = (bf16[80,2432]{1,0:T(8,128)(2,1)}, bf16[80,2432]{1,0:T(8,128)(2,1)}, u32[]{:S(2)}, u32[]{:S(2)}) collective-permute-start(bf16[80,2432]{1,0:T(8,128)(2,1)} %get-tuple-element.14), channel_id=1, source_target_pairs={{0,2},{1,3},{2,0},{3,1},{4,6},{5,7},{6,4},{7,5},{8,10},{9,11},{10,... | collective-permute-start | bytes 1167368 | tf_op jit(solution)/shard_map/ppermute | solution.py:20
  11.7 47.7 %collective-permute-start.6 = (bf16[80,2432]{1,0:T(8,128)(2,1)}, bf16[80,2432]{1,0:T(8,128)(2,1)}, u32[]{:S(2)}, u32[]{:S(2)}) collective-permute-start(bf16[80,2432]{1,0:T(8,128)(2,1)} %get-tuple-element.13), channel_id=1, source_target_pairs={{0,2},{1,3},{2,0},{3,1},{4,6},{5,7},{6,4},{7,5},{8,10},{9,11},{10,... | collective-permute-start | bytes 1167368 | tf_op jit(solution)/shard_map/ppermute | solution.py:20
  72.3 121.8 %collective-permute-start.40 = (bf16[128,2432]{1,0:T(8,128)(2,1)S(1)}, bf16[128,2432]{1,0:T(8,128)(2,1)S(1)}, u32[]{:S(2)}, u32[]{:S(2)}) collective-permute-start(bf16[128,2432]{1,0:T(8,128)(2,1)S(1)} %fusion.21), channel_id=1, source_target_pairs={{4,20},{8,24},{12,28},{20,36},{24,40},{28,44},{36,52},{40,56},{44,... | collective-permute-start | bytes 1867784 | tf_op jit(solution)/shard_map/ppermute | solution.py:26
  78.6 29.7 %collective-permute-start.22 = (bf16[2304,128]{1,0:T(8,128)(2,1)S(1)}, bf16[2304,128]{1,0:T(8,128)(2,1)S(1)}, u32[]{:S(2)}, u32[]{:S(2)}) collective-permute-start(bf16[2304,128]{1,0:T(8,128)(2,1)S(1)} %fusion.18), channel_id=1, source_target_pairs={{4,20},{8,24},{12,28},{20,36},{24,40},{28,44},{36,52},{40,56},{44,... | collective-permute-start | bytes 1769480 | tf_op jit(solution)/shard_map/ppermute | solution.py:26
  83.2 91.9 %collective-permute-start.19 = (bf16[2432,128]{1,0:T(8,128)(2,1)S(1)}, bf16[2432,128]{1,0:T(8,128)(2,1)S(1)}, u32[]{:S(2)}, u32[]{:S(2)}) collective-permute-start(bf16[2432,128]{1,0:T(8,128)(2,1)S(1)} %fusion.23), channel_id=1, source_target_pairs={{4,20},{8,24},{12,28},{20,36},{24,40},{28,44},{36,52},{40,56},{44,... | collective-permute-start | bytes 1867784 | tf_op jit(solution)/shard_map/ppermute | solution.py:26
  87.8 89.4 %collective-permute-start.10 = (bf16[2432,128]{1,0:T(8,128)(2,1)S(1)}, bf16[2432,128]{1,0:T(8,128)(2,1)S(1)}, u32[]{:S(2)}, u32[]{:S(2)}) collective-permute-start(bf16[2432,128]{1,0:T(8,128)(2,1)S(1)} %fusion.22), channel_id=1, source_target_pairs={{4,20},{8,24},{12,28},{20,36},{24,40},{28,44},{36,52},{40,56},{44,... | collective-permute-start | bytes 1867784 | tf_op jit(solution)/shard_map/ppermute | solution.py:26
  93.5 54.1 %collective-permute-start.31 = (bf16[2304,128]{1,0:T(8,128)(2,1)S(1)}, bf16[2304,128]{1,0:T(8,128)(2,1)S(1)}, u32[]{:S(2)}, u32[]{:S(2)}) collective-permute-start(bf16[2304,128]{1,0:T(8,128)(2,1)S(1)} %fusion.19), channel_id=1, source_target_pairs={{4,20},{8,24},{12,28},{20,36},{24,40},{28,44},{36,52},{40,56},{44,... | collective-permute-start | bytes 1769480 | tf_op jit(solution)/shard_map/ppermute | solution.py:26
  108.3 69.0 %collective-permute-start.28 = (bf16[2432,128]{1,0:T(8,128)(2,1)S(1)}, bf16[2432,128]{1,0:T(8,128)(2,1)S(1)}, u32[]{:S(2)}, u32[]{:S(2)}) collective-permute-start(bf16[2432,128]{1,0:T(8,128)(2,1)S(1)} %fusion.25), channel_id=1, source_target_pairs={{4,20},{8,24},{12,28},{20,36},{24,40},{28,44},{36,52},{40,56},{44,... | collective-permute-start | bytes 1867784 | tf_op jit(solution)/shard_map/ppermute | solution.py:26
  175.1 30.8 %collective-permute-start.37 = (bf16[128,2432]{1,0:T(8,128)(2,1)S(1)}, bf16[128,2432]{1,0:T(8,128)(2,1)S(1)}, u32[]{:S(2)}, u32[]{:S(2)}) collective-permute-start(bf16[128,2432]{1,0:T(8,128)(2,1)S(1)} %fusion.26), channel_id=1, source_target_pairs={{4,20},{8,24},{12,28},{20,36},{24,40},{28,44},{36,52},{40,56},{44,... | collective-permute-start | bytes 1867784 | tf_op jit(solution)/shard_map/ppermute | solution.py:26
  177.3 32.3 %collective-permute-start.32 = (bf16[2304,128]{1,0:T(8,128)(2,1)S(1)}, bf16[2304,128]{1,0:T(8,128)(2,1)S(1)}, u32[]{:S(2)}, u32[]{:S(2)}) collective-permute-start(bf16[2304,128]{1,0:T(8,128)(2,1)S(1)} %broadcast_select_fusion.7), channel_id=1, source_target_pairs={{0,12},{4,8},{8,4},{12,0},{16,28},{20,24},{24,20},{28,16},{32,44},... | collective-permute-start | bytes 1769480 | tf_op jit(solution)/shard_map/ppermute | solution.py:26
  194.1 39.2 %collective-permute-start.20 = (bf16[2432,128]{1,0:T(8,128)(2,1)S(1)}, bf16[2432,128]{1,0:T(8,128)(2,1)S(1)}, u32[]{:S(2)}, u32[]{:S(2)}) collective-permute-start(bf16[2432,128]{1,0:T(8,128)(2,1)S(1)} %broadcast_select_fusion.4), channel_id=1, source_target_pairs={{0,12},{4,8},{8,4},{12,0},{16,28},{20,24},{24,20},{28,16},{32,44},... | collective-permute-start | bytes 1867784 | tf_op jit(solution)/shard_map/ppermute | solution.py:26
  205.9 40.7 %collective-permute-start.11 = (bf16[2432,128]{1,0:T(8,128)(2,1)S(1)}, bf16[2432,128]{1,0:T(8,128)(2,1)S(1)}, u32[]{:S(2)}, u32[]{:S(2)}) collective-permute-start(bf16[2432,128]{1,0:T(8,128)(2,1)S(1)} %broadcast_select_fusion.5), channel_id=1, source_target_pairs={{0,12},{4,8},{8,4},{12,0},{16,28},{20,24},{24,20},{28,16},{32,44},... | collective-permute-start | bytes 1867784 | tf_op jit(solution)/shard_map/ppermute | solution.py:26
  206.0 53.9 %collective-permute-start.29 = (bf16[2432,128]{1,0:T(8,128)(2,1)S(1)}, bf16[2432,128]{1,0:T(8,128)(2,1)S(1)}, u32[]{:S(2)}, u32[]{:S(2)}) collective-permute-start(bf16[2432,128]{1,0:T(8,128)(2,1)S(1)} %broadcast_select_fusion.2), channel_id=1, source_target_pairs={{0,12},{4,8},{8,4},{12,0},{16,28},{20,24},{24,20},{28,16},{32,44},... | collective-permute-start | bytes 1867784 | tf_op jit(solution)/shard_map/ppermute | solution.py:26
  209.6 63.6 %collective-permute-start.26 = (bf16[2432,128]{1,0:T(8,128)(2,1)S(1)}, bf16[2432,128]{1,0:T(8,128)(2,1)S(1)}, u32[]{:S(2)}, u32[]{:S(2)}) collective-permute-start(bf16[2432,128]{1,0:T(8,128)(2,1)S(1)} %broadcast_select_fusion.3), channel_id=1, source_target_pairs={{0,12},{4,8},{8,4},{12,0},{16,28},{20,24},{24,20},{28,16},{32,44},... | collective-permute-start | bytes 1867784 | tf_op jit(solution)/shard_map/ppermute | solution.py:26
  219.9 66.7 %collective-permute-start.41 = (bf16[128,2432]{1,0:T(8,128)(2,1)S(1)}, bf16[128,2432]{1,0:T(8,128)(2,1)S(1)}, u32[]{:S(2)}, u32[]{:S(2)}) collective-permute-start(bf16[128,2432]{1,0:T(8,128)(2,1)S(1)} %broadcast_select_fusion), channel_id=1, source_target_pairs={{0,12},{4,8},{8,4},{12,0},{16,28},{20,24},{24,20},{28,16},{32,44},... | collective-permute-start | bytes 1867784 | tf_op jit(solution)/shard_map/ppermute | solution.py:26
  233.2 65.3 %collective-permute-start.38 = (bf16[128,2432]{1,0:T(8,128)(2,1)S(1)}, bf16[128,2432]{1,0:T(8,128)(2,1)S(1)}, u32[]{:S(2)}, u32[]{:S(2)}) collective-permute-start(bf16[128,2432]{1,0:T(8,128)(2,1)S(1)} %broadcast_select_fusion.1), channel_id=1, source_target_pairs={{0,12},{4,8},{8,4},{12,0},{16,28},{20,24},{24,20},{28,16},{32,44},... | collective-permute-start | bytes 1867784 | tf_op jit(solution)/shard_map/ppermute | solution.py:26
  246.6 52.3 %collective-permute-start.24 = (bf16[2304,128]{1,0:T(8,128)(2,1)S(1)}, bf16[2304,128]{1,0:T(8,128)(2,1)S(1)}, u32[]{:S(2)}, u32[]{:S(2)}) collective-permute-start(bf16[2304,128]{1,0:T(8,128)(2,1)S(1)} %fusion.76), channel_id=1, source_target_pairs={{0,4},{4,0},{8,12},{12,8},{16,20},{20,16},{24,28},{28,24},{32,36},... | collective-permute-start | bytes 1769480 | tf_op jit(solution)/shard_map/ppermute | solution.py:26
  259.9 41.4 %collective-permute-start.33 = (bf16[2304,128]{1,0:T(8,128)(2,1)S(1)}, bf16[2304,128]{1,0:T(8,128)(2,1)S(1)}, u32[]{:S(2)}, u32[]{:S(2)}) collective-permute-start(bf16[2304,128]{1,0:T(8,128)(2,1)S(1)} %fusion.82), channel_id=1, source_target_pairs={{0,4},{4,0},{8,12},{12,8},{16,20},{20,16},{24,28},{28,24},{32,36},... | collective-permute-start | bytes 1769480 | tf_op jit(solution)/shard_map/ppermute | solution.py:26
  298.9 29.9 %collective-permute-start.30 = (bf16[2432,128]{1,0:T(8,128)(2,1)S(1)}, bf16[2432,128]{1,0:T(8,128)(2,1)S(1)}, u32[]{:S(2)}, u32[]{:S(2)}) collective-permute-start(bf16[2432,128]{1,0:T(8,128)(2,1)S(1)} %fusion.58), channel_id=1, source_target_pairs={{0,4},{4,0},{8,12},{12,8},{16,20},{20,16},{24,28},{28,24},{32,36},... | collective-permute-start | bytes 1867784 | tf_op jit(solution)/shard_map/ppermute | solution.py:26
  301.3 40.8 %collective-permute-start.27 = (bf16[2432,128]{1,0:T(8,128)(2,1)S(1)}, bf16[2432,128]{1,0:T(8,128)(2,1)S(1)}, u32[]{:S(2)}, u32[]{:S(2)}) collective-permute-start(bf16[2432,128]{1,0:T(8,128)(2,1)S(1)} %fusion.52), channel_id=1, source_target_pairs={{0,4},{4,0},{8,12},{12,8},{16,20},{20,16},{24,28},{28,24},{32,36},... | collective-permute-start | bytes 1867784 | tf_op jit(solution)/shard_map/ppermute | solution.py:26
  301.7 53.7 %collective-permute-start.42 = (bf16[128,2432]{1,0:T(8,128)(2,1)S(1)}, bf16[128,2432]{1,0:T(8,128)(2,1)S(1)}, u32[]{:S(2)}, u32[]{:S(2)}) collective-permute-start(bf16[128,2432]{1,0:T(8,128)(2,1)S(1)} %fusion.70), channel_id=1, source_target_pairs={{0,4},{4,0},{8,12},{12,8},{16,20},{20,16},{24,28},{28,24},{32,36},... | collective-permute-start | bytes 1867784 | tf_op jit(solution)/shard_map/ppermute | solution.py:26
  304.3 62.2 %collective-permute-start.39 = (bf16[128,2432]{1,0:T(8,128)(2,1)S(1)}, bf16[128,2432]{1,0:T(8,128)(2,1)S(1)}, u32[]{:S(2)}, u32[]{:S(2)}) collective-permute-start(bf16[128,2432]{1,0:T(8,128)(2,1)S(1)} %fusion.64), channel_id=1, source_target_pairs={{0,4},{4,0},{8,12},{12,8},{16,20},{20,16},{24,28},{28,24},{32,36},... | collective-permute-start | bytes 1867784 | tf_op jit(solution)/shard_map/ppermute | solution.py:26
  (23 other events, 335.4 us)

commit v2 on v1

--- a/solution.py
+++ b/solution.py
@@ -7,6 +7,7 @@
 step_size = 0.5
 ROW = 4
 DOWN_CUTS = (0, 18, 37, 56)
+GATHER_CUTS = (0, 37, 56)
 GATE_CUTS = (0, 19, 38, 56)
 UP_CUTS = (0, 19, 38, 56)
 
@@ -67,7 +68,8 @@
 
     x2 = swapped(x0, 2)
     x1 = swapped(x0, 1)
-    d2 = [swapped(d0[:, s], 2) for s in spans]
+    halves = cuts(width, GATHER_CUTS)
+    d2 = [swapped(d0[:, s], 2) for s in halves]
     d1 = swapped(d0, 1)
     x3 = swapped(x2, 1)
     d3 = [swapped(d, 1) for d in d2]
@@ -83,12 +85,15 @@
     scale = 0.125 / mass_next[0]
 
     x = jnp.concatenate([x0, x1, x2, x3], axis=0)
-    gate_pre = jnp.dot(x, gate_w, preferred_element_type=f32) * inv_d
-    up_pre = jnp.dot(x, up_w, preferred_element_type=f32) * inv_d
+    both = jnp.concatenate([gate_w, up_w], axis=1)
+    pre = jnp.dot(x, both, preferred_element_type=f32) * inv_d
+    gate_pre = pre[:, :units]
+    up_pre = pre[:, units:]
     sig = jax.nn.sigmoid(gate_pre)
     hidden = (gate_pre * sig * up_pre).astype(bf16)
 
-    dy = [jnp.concatenate([d0[:, s], d1[:, s], d2[c], d3[c]], axis=0) for c, s in enumerate(spans)]
+    dy = [jnp.concatenate([d0[:, s], d1[:, s], d2[c], d3[c]], axis=0) for c, s in enumerate(halves)]
+    dy_spans = [dy[0][:, spans[0]], dy[0][:, spans[1]], dy[1]]
     weight = mass[0]
     rows = (((0,), (0,)), ((), ()))
 
@@ -96,12 +101,12 @@
         grad = lax.dot_general(lhs, rhs, rows, preferred_element_type=f32) * scale_by
         return (weight * (w.astype(f32) - step_size * grad)).astype(bf16)
 
-    down_numer = [numer(down_w[:, s], hidden, dy[c], inv_h) for c, s in enumerate(spans)]
+    down_numer = [numer(down_w[:, s], hidden, dy_spans[c], inv_h) for c, s in enumerate(spans)]
     down_next = [mixed(n, place, scale) for n in down_numer]
     gate_pre, up_pre, _ = lax.optimization_barrier((gate_pre, up_pre, down_numer[-1]))
     sig = jax.nn.sigmoid(gate_pre)
     hidden_grad = 0.0
-    for c, s in enumerate(spans):
+    for c, s in enumerate(halves):
         hidden_grad = hidden_grad + lax.dot_general(
             dy[c], down_w[:, s], (((1,), (1,)), ((), ())), preferred_element_type=f32
         )

time: 376 us -> 346 us (0.920)
  the two profiles are of different devices: /device:TPU:6 before, /device:TPU:2 now
where the time goes in v2:
time: 346 us; the launch traced here: 344 us
  waiting for transfers between devices  235 us (68%)
  starting transfers between devices  72 us (21%)
  matrix products  14.9 us (4%)
  other arithmetic  12.5 us (4%)
  local copies, waits for them, and re-layouts  7.32 us (2%)
    ppermute x27, waiting for transfers between devices, moved(): return lax.ppermute(array, 'blk', pairs)  197 us
    ppermute x27, starting transfers between devices, moved(): return lax.ppermute(array, 'blk', pairs)  48.7 us
    ppermute x8, waiting for transfers between devices, swapped(): return lax.ppermute(array, 'mp', [(i, i ^ mask) for i in range(count)])  30.8 us
    ppermute x6, starting transfers between devices, everyone(): other = lax.ppermute(ring, 'blk', [(r, r ^ bit) for r in range(count)])  16.4 us
    dot_general x9, matrix products, numer(): lax.dot_general(lhs, rhs, rows, preferred_element_type=f32) * scale_by  9.27 us
    ppermute x6, waiting for transfers between devices, everyone(): other = lax.ppermute(ring, 'blk', [(r, r ^ bit) for r in range(count)])  7.78 us
  transfers between devices with their start and end apart: 41, of which 24 were waited for; matrix products, arithmetic and copies ran while one was open for 9% of the time, Pallas kernels for 0%

profile of v2, /device:TPU:2, one launch (start us, length us, event | category | flops | bytes accessed | tf_op | source)
XLA Modules:
  0.0 344.4 jit_solution(9004757907302961377)
XLA Ops:
  0.6 3.3 collective-permute-start.1
  11.8 18.7 %collective-permute-done.1 = bf16[80,7168]{1,0:T(8,128)(2,1)S(1)} collective-permute-done((bf16[80,7168]{1,0:T(8,128)(2,1)}, bf16[80,7168]{1,0:T(8,128)(2,1)S(1)}, u32[]{:S(2)}, u32[]{:S(2)}) %collective-permute-start.1) | collective-permute-done | bytes 1146912 | tf_op jit(solution)/shard_map/ppermute | solution.py:21
  39.1 6.8 %collective-permute-start.15 = (f32[64]{0:T(128)S(1)}, f32[64]{0:T(128)S(1)}, u32[]{:S(2)}, u32[]{:S(2)}) collective-permute-start(f32[64]{0:T(128)S(1)} %add.150), channel_id=1, source_target_pairs={{0,64},{4,68},{8,72},{12,76},{16,80},{20,84},{24,88},{28,92},{32,9... | collective-permute-start | bytes 776 | tf_op jit(solution)/shard_map/ppermute | solution.py:35
  57.6 12.0 %collective-permute-done.4 = bf16[80,4736]{1,0:T(8,128)(2,1)} collective-permute-done((bf16[80,4736]{1,0:T(8,128)(2,1)}, bf16[80,4736]{1,0:T(8,128)(2,1)}, u32[]{:S(2)}, u32[]{:S(2)}) %collective-permute-start.4) | collective-permute-done | bytes 757792 | tf_op jit(solution)/shard_map/ppermute | solution.py:21
  82.2 3.4 collective-permute-start.32
  87.3 3.8 %collective-permute-start.35 = (bf16[128,2432]{1,0:T(8,128)(2,1)S(1)}, bf16[128,2432]{1,0:T(8,128)(2,1)S(1)}, u32[]{:S(2)}, u32[]{:S(2)}) collective-permute-start(bf16[128,2432]{1,0:T(8,128)(2,1)S(1)} %fusion.30), channel_id=1, source_target_pairs={{4,20},{8,24},{12,28},{20,36},{24,40},{28,44},{36,52},{40,56},{44,... | collective-permute-start | bytes 1867784 | tf_op jit(solution)/shard_map/ppermute | solution.py:27
  94.3 5.1 %collective-permute-start.20 = (bf16[2304,128]{1,0:T(8,128)(2,1)S(1)}, bf16[2304,128]{1,0:T(8,128)(2,1)S(1)}, u32[]{:S(2)}, u32[]{:S(2)}) collective-permute-start(bf16[2304,128]{1,0:T(8,128)(2,1)S(1)} %fusion.22), channel_id=1, source_target_pairs={{4,20},{8,24},{12,28},{20,36},{24,40},{28,44},{36,52},{40,56},{44,... | collective-permute-start | bytes 1769480 | tf_op jit(solution)/shard_map/ppermute | solution.py:27
  106.3 5.2 %collective-permute-done.32 = bf16[128,2304]{1,0:T(8,128)(2,1)S(1)} collective-permute-done((bf16[128,2304]{1,0:T(8,128)(2,1)S(1)}, bf16[128,2304]{1,0:T(8,128)(2,1)S(1)}, u32[]{:S(2)}, u32[]{:S(2)}) %collective-permute-start.32) | collective-permute-done | bytes 589856 | tf_op jit(solution)/shard_map/ppermute | solution.py:27
  113.5 24.0 %collective-permute-done.20 = bf16[2304,128]{1,0:T(8,128)(2,1)S(1)} collective-permute-done((bf16[2304,128]{1,0:T(8,128)(2,1)S(1)}, bf16[2304,128]{1,0:T(8,128)(2,1)S(1)}, u32[]{:S(2)}, u32[]{:S(2)}) %collective-permute-start.20) | collective-permute-done | bytes 589856 | tf_op jit(solution)/shard_map/ppermute | solution.py:27
  139.5 10.7 %collective-permute-done.29 = bf16[2304,128]{1,0:T(8,128)(2,1)S(1)} collective-permute-done((bf16[2304,128]{1,0:T(8,128)(2,1)S(1)}, bf16[2304,128]{1,0:T(8,128)(2,1)S(1)}, u32[]{:S(2)}, u32[]{:S(2)}) %collective-permute-start.29) | collective-permute-done | bytes 589856 | tf_op jit(solution)/shard_map/ppermute | solution.py:27
  155.8 7.6 %collective-permute-done.8 = bf16[2432,128]{1,0:T(8,128)(2,1)S(1)} collective-permute-done((bf16[2432,128]{1,0:T(8,128)(2,1)S(1)}, bf16[2432,128]{1,0:T(8,128)(2,1)S(1)}, u32[]{:S(2)}, u32[]{:S(2)}) %collective-permute-start.8) | collective-permute-done | bytes 622624 | tf_op jit(solution)/shard_map/ppermute | solution.py:27
  165.0 11.8 %collective-permute-done.17 = bf16[2432,128]{1,0:T(8,128)(2,1)S(1)} collective-permute-done((bf16[2432,128]{1,0:T(8,128)(2,1)S(1)}, bf16[2432,128]{1,0:T(8,128)(2,1)S(1)}, u32[]{:S(2)}, u32[]{:S(2)}) %collective-permute-start.17) | collective-permute-done | bytes 622624 | tf_op jit(solution)/shard_map/ppermute | solution.py:27
  178.4 11.8 %collective-permute-done.23 = bf16[2432,128]{1,0:T(8,128)(2,1)S(1)} collective-permute-done((bf16[2432,128]{1,0:T(8,128)(2,1)S(1)}, bf16[2432,128]{1,0:T(8,128)(2,1)S(1)}, u32[]{:S(2)}, u32[]{:S(2)}) %collective-permute-start.23) | collective-permute-done | bytes 622624 | tf_op jit(solution)/shard_map/ppermute | solution.py:27
  191.7 11.6 %collective-permute-done.26 = bf16[2432,128]{1,0:T(8,128)(2,1)S(1)} collective-permute-done((bf16[2432,128]{1,0:T(8,128)(2,1)S(1)}, bf16[2432,128]{1,0:T(8,128)(2,1)S(1)}, u32[]{:S(2)}, u32[]{:S(2)}) %collective-permute-start.26) | collective-permute-done | bytes 622624 | tf_op jit(solution)/shard_map/ppermute | solution.py:27
  210.9 11.5 %collective-permute-done.39 = bf16[128,2432]{1,0:T(8,128)(2,1)S(1)} collective-permute-done((bf16[128,2432]{1,0:T(8,128)(2,1)S(1)}, bf16[128,2432]{1,0:T(8,128)(2,1)S(1)}, u32[]{:S(2)}, u32[]{:S(2)}) %collective-permute-start.39) | collective-permute-done | bytes 622624 | tf_op jit(solution)/shard_map/ppermute | solution.py:27
  224.0 11.7 %collective-permute-done.9 = bf16[2432,128]{1,0:T(8,128)(2,1)S(1)} collective-permute-done((bf16[2432,128]{1,0:T(8,128)(2,1)S(1)}, bf16[2432,128]{1,0:T(8,128)(2,1)S(1)}, u32[]{:S(2)}, u32[]{:S(2)}) %collective-permute-start.9) | collective-permute-done | bytes 622624 | tf_op jit(solution)/shard_map/ppermute | solution.py:27
  237.4 11.7 %collective-permute-done.18 = bf16[2432,128]{1,0:T(8,128)(2,1)S(1)} collective-permute-done((bf16[2432,128]{1,0:T(8,128)(2,1)S(1)}, bf16[2432,128]{1,0:T(8,128)(2,1)S(1)}, u32[]{:S(2)}, u32[]{:S(2)}) %collective-permute-start.18) | collective-permute-done | bytes 622624 | tf_op jit(solution)/shard_map/ppermute | solution.py:27
  250.7 11.7 %collective-permute-done.24 = bf16[2432,128]{1,0:T(8,128)(2,1)S(1)} collective-permute-done((bf16[2432,128]{1,0:T(8,128)(2,1)S(1)}, bf16[2432,128]{1,0:T(8,128)(2,1)S(1)}, u32[]{:S(2)}, u32[]{:S(2)}) %collective-permute-start.24) | collective-permute-done | bytes 622624 | tf_op jit(solution)/shard_map/ppermute | solution.py:27
  264.1 10.5 %collective-permute-done.27 = bf16[2432,128]{1,0:T(8,128)(2,1)S(1)} collective-permute-done((bf16[2432,128]{1,0:T(8,128)(2,1)S(1)}, bf16[2432,128]{1,0:T(8,128)(2,1)S(1)}, u32[]{:S(2)}, u32[]{:S(2)}) %collective-permute-start.27) | collective-permute-done | bytes 622624 | tf_op jit(solution)/shard_map/ppermute | solution.py:27
  282.2 9.3 %collective-permute-done.40 = bf16[128,2432]{1,0:T(8,128)(2,1)S(1)} collective-permute-done((bf16[128,2432]{1,0:T(8,128)(2,1)S(1)}, bf16[128,2432]{1,0:T(8,128)(2,1)S(1)}, u32[]{:S(2)}, u32[]{:S(2)}) %collective-permute-start.40) | collective-permute-done | bytes 622624 | tf_op jit(solution)/shard_map/ppermute | solution.py:27
  293.2 11.6 %collective-permute-done.10 = bf16[2432,128]{1,0:T(8,128)(2,1)S(1)} collective-permute-done((bf16[2432,128]{1,0:T(8,128)(2,1)S(1)}, bf16[2432,128]{1,0:T(8,128)(2,1)S(1)}, u32[]{:S(2)}, u32[]{:S(2)}) %collective-permute-start.10) | collective-permute-done | bytes 622624 | tf_op jit(solution)/shard_map/ppermute | solution.py:27
  305.1 13.0 %collective-permute-done.19 = bf16[2432,128]{1,0:T(8,128)(2,1)S(1)} collective-permute-done((bf16[2432,128]{1,0:T(8,128)(2,1)S(1)}, bf16[2432,128]{1,0:T(8,128)(2,1)S(1)}, u32[]{:S(2)}, u32[]{:S(2)}) %collective-permute-start.19) | collective-permute-done | bytes 622624 | tf_op jit(solution)/shard_map/ppermute | solution.py:27
  319.8 11.7 %collective-permute-done.25 = bf16[2432,128]{1,0:T(8,128)(2,1)S(1)} collective-permute-done((bf16[2432,128]{1,0:T(8,128)(2,1)S(1)}, bf16[2432,128]{1,0:T(8,128)(2,1)S(1)}, u32[]{:S(2)}, u32[]{:S(2)}) %collective-permute-start.25) | collective-permute-done | bytes 622624 | tf_op jit(solution)/shard_map/ppermute | solution.py:27
  331.8 11.0 %collective-permute-done.28 = bf16[2432,128]{1,0:T(8,128)(2,1)S(1)} collective-permute-done((bf16[2432,128]{1,0:T(8,128)(2,1)S(1)}, bf16[2432,128]{1,0:T(8,128)(2,1)S(1)}, u32[]{:S(2)}, u32[]{:S(2)}) %collective-permute-start.28) | collective-permute-done | bytes 622624 | tf_op jit(solution)/shard_map/ppermute | solution.py:27
  (131 shorter events, 92.6 us)
Async XLA Ops:
  5.2 64.4 %collective-permute-start.3 = (bf16[80,7168]{1,0:T(8,128)(2,1)}, bf16[80,7168]{1,0:T(8,128)(2,1)}, u32[]{:S(2)}, u32[]{:S(2)}) collective-permute-start(bf16[80,7168]{1,0:T(8,128)(2,1)} %bitcast.62), channel_id=1, source_target_pairs={{0,1},{1,0},{2,3},{3,2},{4,5},{5,4},{6,7},{7,6},{8,9},{9,8},{10,11... | collective-permute-start | bytes 3440648 | tf_op jit(solution)/shard_map/ppermute | solution.py:21
  10.4 63.4 %collective-permute-start = (bf16[80,7168]{1,0:T(8,128)(2,1)}, bf16[80,7168]{1,0:T(8,128)(2,1)S(1)}, u32[]{:S(2)}, u32[]{:S(2)}) collective-permute-start(bf16[80,7168]{1,0:T(8,128)(2,1)} %bitcast.58), channel_id=1, source_target_pairs={{0,1},{1,0},{2,3},{3,2},{4,5},{5,4},{6,7},{7,6},{8,9},{9,8},{10,11... | collective-permute-start | bytes 3440648 | tf_op jit(solution)/shard_map/ppermute | solution.py:21
  11.4 42.8 %collective-permute-start.6 = (bf16[80,2432]{1,0:T(8,128)(2,1)S(1)}, bf16[80,2432]{1,0:T(8,128)(2,1)}, u32[]{:S(2)}, u32[]{:S(2)}) collective-permute-start(bf16[80,2432]{1,0:T(8,128)(2,1)S(1)} %slice.130), channel_id=1, source_target_pairs={{0,2},{1,3},{2,0},{3,1},{4,6},{5,7},{6,4},{7,5},{8,10},{9,11},{10,... | collective-permute-start | bytes 1167368 | tf_op jit(solution)/shard_map/ppermute | solution.py:21
  30.6 43.2 %collective-permute-start.2 = (bf16[80,7168]{1,0:T(8,128)(2,1)S(1)}, bf16[80,7168]{1,0:T(8,128)(2,1)S(1)}, u32[]{:S(2)}, u32[]{:S(2)}) collective-permute-start(bf16[80,7168]{1,0:T(8,128)(2,1)S(1)} %collective-permute-done.1), channel_id=1, source_target_pairs={{0,1},{1,0},{2,3},{3,2},{4,5},{5,4},{6,7},{7,6},{8,9},{9,8},{10,11... | collective-permute-start | bytes 3440648 | tf_op jit(solution)/shard_map/ppermute | solution.py:21
  77.7 76.5 %collective-permute-start.38 = (bf16[128,2432]{1,0:T(8,128)(2,1)S(1)}, bf16[128,2432]{1,0:T(8,128)(2,1)S(1)}, u32[]{:S(2)}, u32[]{:S(2)}) collective-permute-start(bf16[128,2432]{1,0:T(8,128)(2,1)S(1)} %fusion.25), channel_id=1, source_target_pairs={{4,20},{8,24},{12,28},{20,36},{24,40},{28,44},{36,52},{40,56},{44,... | collective-permute-start | bytes 1867784 | tf_op jit(solution)/shard_map/ppermute | solution.py:27
  87.3 64.8 %collective-permute-start.35 = (bf16[128,2432]{1,0:T(8,128)(2,1)S(1)}, bf16[128,2432]{1,0:T(8,128)(2,1)S(1)}, u32[]{:S(2)}, u32[]{:S(2)}) collective-permute-start(bf16[128,2432]{1,0:T(8,128)(2,1)S(1)} %fusion.30), channel_id=1, source_target_pairs={{4,20},{8,24},{12,28},{20,36},{24,40},{28,44},{36,52},{40,56},{44,... | collective-permute-start | bytes 1867784 | tf_op jit(solution)/shard_map/ppermute | solution.py:27
  94.3 43.1 %collective-permute-start.20 = (bf16[2304,128]{1,0:T(8,128)(2,1)S(1)}, bf16[2304,128]{1,0:T(8,128)(2,1)S(1)}, u32[]{:S(2)}, u32[]{:S(2)}) collective-permute-start(bf16[2304,128]{1,0:T(8,128)(2,1)S(1)} %fusion.22), channel_id=1, source_target_pairs={{4,20},{8,24},{12,28},{20,36},{24,40},{28,44},{36,52},{40,56},{44,... | collective-permute-start | bytes 1769480 | tf_op jit(solution)/shard_map/ppermute | solution.py:27
  100.1 50.0 %collective-permute-start.29 = (bf16[2304,128]{1,0:T(8,128)(2,1)S(1)}, bf16[2304,128]{1,0:T(8,128)(2,1)S(1)}, u32[]{:S(2)}, u32[]{:S(2)}) collective-permute-start(bf16[2304,128]{1,0:T(8,128)(2,1)S(1)} %fusion.23), channel_id=1, source_target_pairs={{4,20},{8,24},{12,28},{20,36},{24,40},{28,44},{36,52},{40,56},{44,... | collective-permute-start | bytes 1769480 | tf_op jit(solution)/shard_map/ppermute | solution.py:27
  111.5 52.0 %collective-permute-start.8 = (bf16[2432,128]{1,0:T(8,128)(2,1)S(1)}, bf16[2432,128]{1,0:T(8,128)(2,1)S(1)}, u32[]{:S(2)}, u32[]{:S(2)}) collective-permute-start(bf16[2432,128]{1,0:T(8,128)(2,1)S(1)} %fusion.26), channel_id=1, source_target_pairs={{4,20},{8,24},{12,28},{20,36},{24,40},{28,44},{36,52},{40,56},{44,... | collective-permute-start | bytes 1867784 | tf_op jit(solution)/shard_map/ppermute | solution.py:27
  137.5 39.3 %collective-permute-start.17 = (bf16[2432,128]{1,0:T(8,128)(2,1)S(1)}, bf16[2432,128]{1,0:T(8,128)(2,1)S(1)}, u32[]{:S(2)}, u32[]{:S(2)}) collective-permute-start(bf16[2432,128]{1,0:T(8,128)(2,1)S(1)} %fusion.27), channel_id=1, source_target_pairs={{4,20},{8,24},{12,28},{20,36},{24,40},{28,44},{36,52},{40,56},{44,... | collective-permute-start | bytes 1867784 | tf_op jit(solution)/shard_map/ppermute | solution.py:27
  150.1 40.0 %collective-permute-start.23 = (bf16[2432,128]{1,0:T(8,128)(2,1)S(1)}, bf16[2432,128]{1,0:T(8,128)(2,1)S(1)}, u32[]{:S(2)}, u32[]{:S(2)}) collective-permute-start(bf16[2432,128]{1,0:T(8,128)(2,1)S(1)} %fusion.28), channel_id=1, source_target_pairs={{4,20},{8,24},{12,28},{20,36},{24,40},{28,44},{36,52},{40,56},{44,... | collective-permute-start | bytes 1867784 | tf_op jit(solution)/shard_map/ppermute | solution.py:27
  152.1 51.2 %collective-permute-start.26 = (bf16[2432,128]{1,0:T(8,128)(2,1)S(1)}, bf16[2432,128]{1,0:T(8,128)(2,1)S(1)}, u32[]{:S(2)}, u32[]{:S(2)}) collective-permute-start(bf16[2432,128]{1,0:T(8,128)(2,1)S(1)} %fusion.29), channel_id=1, source_target_pairs={{4,20},{8,24},{12,28},{20,36},{24,40},{28,44},{36,52},{40,56},{44,... | collective-permute-start | bytes 1867784 | tf_op jit(solution)/shard_map/ppermute | solution.py:27
  154.2 50.7 %collective-permute-start.33 = (bf16[128,2304]{1,0:T(8,128)(2,1)S(1)}, bf16[128,2304]{1,0:T(8,128)(2,1)S(1)}, u32[]{:S(2)}, u32[]{:S(2)}) collective-permute-start(bf16[128,2304]{1,0:T(8,128)(2,1)S(1)} %broadcast_select_fusion.6), channel_id=1, source_target_pairs={{0,12},{4,8},{8,4},{12,0},{16,28},{20,24},{24,20},{28,16},{32,44},... | collective-permute-start | bytes 1769480 | tf_op jit(solution)/shard_map/ppermute | solution.py:27
  163.4 42.3 %collective-permute-start.21 = (bf16[2304,128]{1,0:T(8,128)(2,1)S(1)}, bf16[2304,128]{1,0:T(8,128)(2,1)S(1)}, u32[]{:S(2)}, u32[]{:S(2)}) collective-permute-start(bf16[2304,128]{1,0:T(8,128)(2,1)S(1)} %broadcast_select_fusion.8), channel_id=1, source_target_pairs={{0,12},{4,8},{8,4},{12,0},{16,28},{20,24},{24,20},{28,16},{32,44},... | collective-permute-start | bytes 1769480 | tf_op jit(solution)/shard_map/ppermute | solution.py:27
  176.8 30.9 %collective-permute-start.30 = (bf16[2304,128]{1,0:T(8,128)(2,1)S(1)}, bf16[2304,128]{1,0:T(8,128)(2,1)S(1)}, u32[]{:S(2)}, u32[]{:S(2)}) collective-permute-start(bf16[2304,128]{1,0:T(8,128)(2,1)S(1)} %broadcast_select_fusion.7), channel_id=1, source_target_pairs={{0,12},{4,8},{8,4},{12,0},{16,28},{20,24},{24,20},{28,16},{32,44},... | collective-permute-start | bytes 1769480 | tf_op jit(solution)/shard_map/ppermute | solution.py:27
  204.9 30.9 %collective-permute-start.9 = (bf16[2432,128]{1,0:T(8,128)(2,1)S(1)}, bf16[2432,128]{1,0:T(8,128)(2,1)S(1)}, u32[]{:S(2)}, u32[]{:S(2)}) collective-permute-start(bf16[2432,128]{1,0:T(8,128)(2,1)S(1)} %broadcast_select_fusion.5), channel_id=1, source_target_pairs={{0,12},{4,8},{8,4},{12,0},{16,28},{20,24},{24,20},{28,16},{32,44},... | collective-permute-start | bytes 1867784 | tf_op jit(solution)/shard_map/ppermute | solution.py:27
  205.8 43.3 %collective-permute-start.18 = (bf16[2432,128]{1,0:T(8,128)(2,1)S(1)}, bf16[2432,128]{1,0:T(8,128)(2,1)S(1)}, u32[]{:S(2)}, u32[]{:S(2)}) collective-permute-start(bf16[2432,128]{1,0:T(8,128)(2,1)S(1)} %broadcast_select_fusion.4), channel_id=1, source_target_pairs={{0,12},{4,8},{8,4},{12,0},{16,28},{20,24},{24,20},{28,16},{32,44},... | collective-permute-start | bytes 1867784 | tf_op jit(solution)/shard_map/ppermute | solution.py:27
  207.7 54.8 %collective-permute-start.24 = (bf16[2432,128]{1,0:T(8,128)(2,1)S(1)}, bf16[2432,128]{1,0:T(8,128)(2,1)S(1)}, u32[]{:S(2)}, u32[]{:S(2)}) collective-permute-start(bf16[2432,128]{1,0:T(8,128)(2,1)S(1)} %broadcast_select_fusion.3), channel_id=1, source_target_pairs={{0,12},{4,8},{8,4},{12,0},{16,28},{20,24},{24,20},{28,16},{32,44},... | collective-permute-start | bytes 1867784 | tf_op jit(solution)/shard_map/ppermute | solution.py:27
  209.1 65.4 %collective-permute-start.27 = (bf16[2432,128]{1,0:T(8,128)(2,1)S(1)}, bf16[2432,128]{1,0:T(8,128)(2,1)S(1)}, u32[]{:S(2)}, u32[]{:S(2)}) collective-permute-start(bf16[2432,128]{1,0:T(8,128)(2,1)S(1)} %broadcast_select_fusion.2), channel_id=1, source_target_pairs={{0,12},{4,8},{8,4},{12,0},{16,28},{20,24},{24,20},{28,16},{32,44},... | collective-permute-start | bytes 1867784 | tf_op jit(solution)/shard_map/ppermute | solution.py:27
  222.4 54.0 %collective-permute-start.34 = (bf16[128,2304]{1,0:T(8,128)(2,1)S(1)}, bf16[128,2304]{1,0:T(8,128)(2,1)S(1)}, u32[]{:S(2)}, u32[]{:S(2)}) collective-permute-start(bf16[128,2304]{1,0:T(8,128)(2,1)S(1)} %fusion.111), channel_id=1, source_target_pairs={{0,4},{4,0},{8,12},{12,8},{16,20},{20,16},{24,28},{28,24},{32,36},... | collective-permute-start | bytes 1769480 | tf_op jit(solution)/shard_map/ppermute | solution.py:27
  235.8 41.5 %collective-permute-start.22 = (bf16[2304,128]{1,0:T(8,128)(2,1)S(1)}, bf16[2304,128]{1,0:T(8,128)(2,1)S(1)}, u32[]{:S(2)}, u32[]{:S(2)}) collective-permute-start(bf16[2304,128]{1,0:T(8,128)(2,1)S(1)} %fusion.99), channel_id=1, source_target_pairs={{0,4},{4,0},{8,12},{12,8},{16,20},{20,16},{24,28},{28,24},{32,36},... | collective-permute-start | bytes 1769480 | tf_op jit(solution)/shard_map/ppermute | solution.py:27
  277.3 40.8 %collective-permute-start.19 = (bf16[2432,128]{1,0:T(8,128)(2,1)S(1)}, bf16[2432,128]{1,0:T(8,128)(2,1)S(1)}, u32[]{:S(2)}, u32[]{:S(2)}) collective-permute-start(bf16[2432,128]{1,0:T(8,128)(2,1)S(1)} %fusion.68), channel_id=1, source_target_pairs={{0,4},{4,0},{8,12},{12,8},{16,20},{20,16},{24,28},{28,24},{32,36},... | collective-permute-start | bytes 1867784 | tf_op jit(solution)/shard_map/ppermute | solution.py:27
  279.3 52.2 %collective-permute-start.25 = (bf16[2432,128]{1,0:T(8,128)(2,1)S(1)}, bf16[2432,128]{1,0:T(8,128)(2,1)S(1)}, u32[]{:S(2)}, u32[]{:S(2)}) collective-permute-start(bf16[2432,128]{1,0:T(8,128)(2,1)S(1)} %fusion.74), channel_id=1, source_target_pairs={{0,4},{4,0},{8,12},{12,8},{16,20},{20,16},{24,28},{28,24},{32,36},... | collective-permute-start | bytes 1867784 | tf_op jit(solution)/shard_map/ppermute | solution.py:27
  280.2 62.6 %collective-permute-start.28 = (bf16[2432,128]{1,0:T(8,128)(2,1)S(1)}, bf16[2432,128]{1,0:T(8,128)(2,1)S(1)}, u32[]{:S(2)}, u32[]{:S(2)}) collective-permute-start(bf16[2432,128]{1,0:T(8,128)(2,1)S(1)} %fusion.80), channel_id=1, source_target_pairs={{0,4},{4,0},{8,12},{12,8},{16,20},{20,16},{24,28},{28,24},{32,36},... | collective-permute-start | bytes 1867784 | tf_op jit(solution)/shard_map/ppermute | solution.py:27
  (23 other events, 344.9 us)

commit v3 on v2

--- a/solution.py
+++ b/solution.py
@@ -5,6 +5,7 @@
 
 
 step_size = 0.5
+PIECES = 3
 ROW = 4
 DOWN_CUTS = (0, 18, 37, 56)
 GATHER_CUTS = (0, 37, 56)
@@ -37,10 +38,10 @@
     return ring
 
 
-def mixed(numer, place, scale):
+def mixed(t, numer, place, scale):
     f32 = jnp.float32
     even = place % 2 == 0
-    above = moved(numer, (None, 4, 4, 4))
+    above = moved(numer, (4, 4, 4, 4) if t == 0 else (None, 4, 4, 4))
     crossing = jnp.where(place < 2, numer, above)
     got = moved(crossing, (3, 1, -1, -3))
     part = jnp.where(even, 3.0 * numer.astype(f32), above.astype(f32)) + 3.0 * got.astype(f32)
@@ -67,10 +68,9 @@
     up_spans = cuts(width, UP_CUTS)
 
     x2 = swapped(x0, 2)
-    x1 = swapped(x0, 1)
+    x1, d1 = jnp.split(swapped(jnp.concatenate([x0, d0], axis=0), 1), 2)
     halves = cuts(width, GATHER_CUTS)
     d2 = [swapped(d0[:, s], 2) for s in halves]
-    d1 = swapped(d0, 1)
     x3 = swapped(x2, 1)
     d3 = [swapped(d, 1) for d in d2]
 
@@ -102,7 +102,7 @@
         return (weight * (w.astype(f32) - step_size * grad)).astype(bf16)
 
     down_numer = [numer(down_w[:, s], hidden, dy_spans[c], inv_h) for c, s in enumerate(spans)]
-    down_next = [mixed(n, place, scale) for n in down_numer]
+    down_next = [mixed(c, n, place, scale) for c, n in enumerate(down_numer)]
     gate_pre, up_pre, _ = lax.optimization_barrier((gate_pre, up_pre, down_numer[-1]))
     sig = jax.nn.sigmoid(gate_pre)
     hidden_grad = 0.0
@@ -113,8 +113,14 @@
     hidden_grad = hidden_grad * inv_h
     gate_gp = (hidden_grad * up_pre * sig * (1.0 + gate_pre * (1.0 - sig))).astype(bf16)
     up_gp = (hidden_grad * gate_pre * sig).astype(bf16)
-    gate_next = [mixed(numer(gate_w[s], x[:, s], gate_gp, inv_d), place, scale) for s in gate_spans]
-    up_next = [mixed(numer(up_w[s], x[:, s], up_gp, inv_d), place, scale) for s in up_spans]
+    gate_next = [
+        mixed(PIECES + c, numer(gate_w[s], x[:, s], gate_gp, inv_d), place, scale)
+        for c, s in enumerate(gate_spans)
+    ]
+    up_next = [
+        mixed(2 * PIECES + c, numer(up_w[s], x[:, s], up_gp, inv_d), place, scale)
+        for c, s in enumerate(up_spans)
+    ]
     return (
         jnp.concatenate(gate_next, axis=0)[None],
         jnp.concatenate(up_next, axis=0)[None],

time: 346 us -> 346 us (level)
  waiting for transfers between devices: 235 us -> 228 us
  other arithmetic: 12.5 us -> 18.1 us
    ppermute x27, waiting for transfers between devices: 197 us -> 191 us  [moved(): return lax.ppermute(array, 'blk', pairs)]
    ppermute x8 -> x7, waiting for transfers between devices: 30.8 us -> 26 us  [swapped(): return lax.ppermute(array, 'mp', [(i, i ^ mask) for i in range(count)])]
    ppermute x8 -> x7, starting transfers between devices: 6.86 us -> 9.02 us  [swapped(): return lax.ppermute(array, 'mp', [(i, i ^ mask) for i in range(count)])]
  transfers between devices with their start and end apart: 41 -> 40, of which waited for: 24 -> 25; matrix products, arithmetic and copies ran while one was open for 9% -> 11% of each run, Pallas kernels for 0% -> 0%
where the time goes in v3:
time: 346 us; the launch traced here: 344 us
  waiting for transfers between devices  228 us (66%)
  starting transfers between devices  71.9 us (21%)
  other arithmetic  18.1 us (5%)
  matrix products  16.9 us (5%)
  local copies, waits for them, and re-layouts  6.56 us (2%)
    ppermute x27, waiting for transfers between devices, moved(): return lax.ppermute(array, 'blk', pairs)  191 us
    ppermute x27, starting transfers between devices, moved(): return lax.ppermute(array, 'blk', pairs)  47.4 us
    ppermute x7, waiting for transfers between devices, swapped(): return lax.ppermute(array, 'mp', [(i, i ^ mask) for i in range(count)])  26 us
    ppermute x6, starting transfers between devices, everyone(): other = lax.ppermute(ring, 'blk', [(r, r ^ bit) for r in range(count)])  15.5 us
    ppermute x6, waiting for transfers between devices, everyone(): other = lax.ppermute(ring, 'blk', [(r, r ^ bit) for r in range(count)])  10.8 us
    dot_general x9, matrix products, numer(): lax.dot_general(lhs, rhs, rows, preferred_element_type=f32) * scale_by  9.29 us
    ppermute x7, starting transfers between devices, swapped(): return lax.ppermute(array, 'mp', [(i, i ^ mask) for i in range(count)])  9.02 us
  transfers between devices with their start and end apart: 40, of which 25 were waited for; matrix products, arithmetic and copies ran while one was open for 11% of the time, Pallas kernels for 0%

profile of v3, /device:TPU:2, one launch (start us, length us, event | category | flops | bytes accessed | tf_op | source)
XLA Modules:
  0.0 344.1 jit_solution(7264811151551746913)
XLA Ops:
  0.7 3.3 pad_maximum_fusion.1
  4.0 3.2 collective-permute-start.1
  7.2 26.0 %collective-permute-done.1 = bf16[80,7168]{1,0:T(8,128)(2,1)S(1)} collective-permute-done((bf16[80,7168]{1,0:T(8,128)(2,1)S(1)}, bf16[80,7168]{1,0:T(8,128)(2,1)S(1)}, u32[]{:S(2)}, u32[]{:S(2)}) %collective-permute-start.1) | collective-permute-done | bytes 1146912 | tf_op jit(solution)/shard_map/ppermute | solution.py:22
  50.3 3.3 collective-permute-start.13
  55.1 6.8 %collective-permute-start.14 = (f32[64]{0:T(128)S(1)}, f32[64]{0:T(128)S(1)}, u32[]{:S(2)}, u32[]{:S(2)}) collective-permute-start(f32[64]{0:T(128)S(1)} %add.150), channel_id=1, source_target_pairs={{0,64},{4,68},{8,72},{12,76},{16,80},{20,84},{24,88},{28,92},{32,9... | collective-permute-start | bytes 776 | tf_op jit(solution)/shard_map/ppermute | solution.py:36
  72.3 3.4 fusion.112
  87.6 4.0 %collective-permute-start.34 = (bf16[128,2432]{1,0:T(8,128)(2,1)S(1)}, bf16[128,2432]{1,0:T(8,128)(2,1)S(1)}, u32[]{:S(2)}, u32[]{:S(2)}) collective-permute-start(bf16[128,2432]{1,0:T(8,128)(2,1)S(1)} %fusion.30), channel_id=1, source_target_pairs={{4,20},{8,24},{12,28},{20,36},{24,40},{28,44},{36,52},{40,56},{44,... | collective-permute-start | bytes 1867784 | tf_op jit(solution)/shard_map/ppermute | solution.py:28
  97.7 5.0 %collective-permute-start.19 = (bf16[2304,128]{1,0:T(8,128)(2,1)S(1)}, bf16[2304,128]{1,0:T(8,128)(2,1)S(1)}, u32[]{:S(2)}, u32[]{:S(2)}) collective-permute-start(bf16[2304,128]{1,0:T(8,128)(2,1)S(1)} %fusion.22), channel_id=1, source_target_pairs={{4,20},{8,24},{12,28},{20,36},{24,40},{28,44},{36,52},{40,56},{44,... | collective-permute-start | bytes 1769480 | tf_op jit(solution)/shard_map/ppermute | solution.py:28
  114.7 24.0 %collective-permute-done.19 = bf16[2304,128]{1,0:T(8,128)(2,1)S(1)} collective-permute-done((bf16[2304,128]{1,0:T(8,128)(2,1)S(1)}, bf16[2304,128]{1,0:T(8,128)(2,1)S(1)}, u32[]{:S(2)}, u32[]{:S(2)}) %collective-permute-start.19) | collective-permute-done | bytes 589856 | tf_op jit(solution)/shard_map/ppermute | solution.py:28
  140.6 10.7 %collective-permute-done.28 = bf16[2304,128]{1,0:T(8,128)(2,1)S(1)} collective-permute-done((bf16[2304,128]{1,0:T(8,128)(2,1)S(1)}, bf16[2304,128]{1,0:T(8,128)(2,1)S(1)}, u32[]{:S(2)}, u32[]{:S(2)}) %collective-permute-start.28) | collective-permute-done | bytes 589856 | tf_op jit(solution)/shard_map/ppermute | solution.py:28
  157.0 7.6 %collective-permute-done.7 = bf16[2432,128]{1,0:T(8,128)(2,1)S(1)} collective-permute-done((bf16[2432,128]{1,0:T(8,128)(2,1)S(1)}, bf16[2432,128]{1,0:T(8,128)(2,1)S(1)}, u32[]{:S(2)}, u32[]{:S(2)}) %collective-permute-start.7) | collective-permute-done | bytes 622624 | tf_op jit(solution)/shard_map/ppermute | solution.py:28
  166.2 11.8 %collective-permute-done.16 = bf16[2432,128]{1,0:T(8,128)(2,1)S(1)} collective-permute-done((bf16[2432,128]{1,0:T(8,128)(2,1)S(1)}, bf16[2432,128]{1,0:T(8,128)(2,1)S(1)}, u32[]{:S(2)}, u32[]{:S(2)}) %collective-permute-start.16) | collective-permute-done | bytes 622624 | tf_op jit(solution)/shard_map/ppermute | solution.py:28
  179.6 11.8 %collective-permute-done.22 = bf16[2432,128]{1,0:T(8,128)(2,1)S(1)} collective-permute-done((bf16[2432,128]{1,0:T(8,128)(2,1)S(1)}, bf16[2432,128]{1,0:T(8,128)(2,1)S(1)}, u32[]{:S(2)}, u32[]{:S(2)}) %collective-permute-start.22) | collective-permute-done | bytes 622624 | tf_op jit(solution)/shard_map/ppermute | solution.py:28
  192.9 11.2 %collective-permute-done.25 = bf16[2432,128]{1,0:T(8,128)(2,1)S(1)} collective-permute-done((bf16[2432,128]{1,0:T(8,128)(2,1)S(1)}, bf16[2432,128]{1,0:T(8,128)(2,1)S(1)}, u32[]{:S(2)}, u32[]{:S(2)}) %collective-permute-start.25) | collective-permute-done | bytes 622624 | tf_op jit(solution)/shard_map/ppermute | solution.py:28
  212.0 11.5 %collective-permute-done.38 = bf16[128,2432]{1,0:T(8,128)(2,1)S(1)} collective-permute-done((bf16[128,2432]{1,0:T(8,128)(2,1)S(1)}, bf16[128,2432]{1,0:T(8,128)(2,1)S(1)}, u32[]{:S(2)}, u32[]{:S(2)}) %collective-permute-start.38) | collective-permute-done | bytes 622624 | tf_op jit(solution)/shard_map/ppermute | solution.py:28
  225.2 11.7 %collective-permute-done.8 = bf16[2432,128]{1,0:T(8,128)(2,1)S(1)} collective-permute-done((bf16[2432,128]{1,0:T(8,128)(2,1)S(1)}, bf16[2432,128]{1,0:T(8,128)(2,1)S(1)}, u32[]{:S(2)}, u32[]{:S(2)}) %collective-permute-start.8) | collective-permute-done | bytes 622624 | tf_op jit(solution)/shard_map/ppermute | solution.py:28
  238.6 11.6 %collective-permute-done.17 = bf16[2432,128]{1,0:T(8,128)(2,1)S(1)} collective-permute-done((bf16[2432,128]{1,0:T(8,128)(2,1)S(1)}, bf16[2432,128]{1,0:T(8,128)(2,1)S(1)}, u32[]{:S(2)}, u32[]{:S(2)}) %collective-permute-start.17) | collective-permute-done | bytes 622624 | tf_op jit(solution)/shard_map/ppermute | solution.py:28
  251.9 11.6 %collective-permute-done.23 = bf16[2432,128]{1,0:T(8,128)(2,1)S(1)} collective-permute-done((bf16[2432,128]{1,0:T(8,128)(2,1)S(1)}, bf16[2432,128]{1,0:T(8,128)(2,1)S(1)}, u32[]{:S(2)}, u32[]{:S(2)}) %collective-permute-start.23) | collective-permute-done | bytes 622624 | tf_op jit(solution)/shard_map/ppermute | solution.py:28
  265.2 9.7 %collective-permute-done.26 = bf16[2432,128]{1,0:T(8,128)(2,1)S(1)} collective-permute-done((bf16[2432,128]{1,0:T(8,128)(2,1)S(1)}, bf16[2432,128]{1,0:T(8,128)(2,1)S(1)}, u32[]{:S(2)}, u32[]{:S(2)}) %collective-permute-start.26) | collective-permute-done | bytes 622624 | tf_op jit(solution)/shard_map/ppermute | solution.py:28
  282.5 9.3 %collective-permute-done.39 = bf16[128,2432]{1,0:T(8,128)(2,1)S(1)} collective-permute-done((bf16[128,2432]{1,0:T(8,128)(2,1)S(1)}, bf16[128,2432]{1,0:T(8,128)(2,1)S(1)}, u32[]{:S(2)}, u32[]{:S(2)}) %collective-permute-start.39) | collective-permute-done | bytes 622624 | tf_op jit(solution)/shard_map/ppermute | solution.py:28
  293.6 11.6 %collective-permute-done.9 = bf16[2432,128]{1,0:T(8,128)(2,1)S(1)} collective-permute-done((bf16[2432,128]{1,0:T(8,128)(2,1)S(1)}, bf16[2432,128]{1,0:T(8,128)(2,1)S(1)}, u32[]{:S(2)}, u32[]{:S(2)}) %collective-permute-start.9) | collective-permute-done | bytes 622624 | tf_op jit(solution)/shard_map/ppermute | solution.py:28
  305.5 13.0 %collective-permute-done.18 = bf16[2432,128]{1,0:T(8,128)(2,1)S(1)} collective-permute-done((bf16[2432,128]{1,0:T(8,128)(2,1)S(1)}, bf16[2432,128]{1,0:T(8,128)(2,1)S(1)}, u32[]{:S(2)}, u32[]{:S(2)}) %collective-permute-start.18) | collective-permute-done | bytes 622624 | tf_op jit(solution)/shard_map/ppermute | solution.py:28
  320.2 11.7 %collective-permute-done.24 = bf16[2432,128]{1,0:T(8,128)(2,1)S(1)} collective-permute-done((bf16[2432,128]{1,0:T(8,128)(2,1)S(1)}, bf16[2432,128]{1,0:T(8,128)(2,1)S(1)}, u32[]{:S(2)}, u32[]{:S(2)}) %collective-permute-start.24) | collective-permute-done | bytes 622624 | tf_op jit(solution)/shard_map/ppermute | solution.py:28
  332.2 10.2 %collective-permute-done.27 = bf16[2432,128]{1,0:T(8,128)(2,1)S(1)} collective-permute-done((bf16[2432,128]{1,0:T(8,128)(2,1)S(1)}, bf16[2432,128]{1,0:T(8,128)(2,1)S(1)}, u32[]{:S(2)}, u32[]{:S(2)}) %collective-permute-start.27) | collective-permute-done | bytes 622624 | tf_op jit(solution)/shard_map/ppermute | solution.py:28
  (129 shorter events, 97.7 us)
Async XLA Ops:
  4.0 67.0 %collective-permute-start = (bf16[160,7168]{1,0:T(8,128)(2,1)}, bf16[160,7168]{1,0:T(8,128)(2,1)}, u32[]{:S(2)}, u32[]{:S(2)}) collective-permute-start(bf16[160,7168]{1,0:T(8,128)(2,1)} %pad_maximum_fusion.1), channel_id=1, source_target_pairs={{0,1},{1,0},{2,3},{3,2},{4,5},{5,4},{6,7},{7,6},{8,9},{9,8},{10,11... | collective-permute-start | bytes 6881288 | tf_op jit(solution)/shard_map/ppermute | solution.py:22
  33.1 39.2 %collective-permute-start.2 = (bf16[80,7168]{1,0:T(8,128)(2,1)S(1)}, bf16[80,7168]{1,0:T(8,128)(2,1)}, u32[]{:S(2)}, u32[]{:S(2)}) collective-permute-start(bf16[80,7168]{1,0:T(8,128)(2,1)S(1)} %collective-permute-done.1), channel_id=1, source_target_pairs={{0,1},{1,0},{2,3},{3,2},{4,5},{5,4},{6,7},{7,6},{8,9},{9,8},{10,11... | collective-permute-start | bytes 3440648 | tf_op jit(solution)/shard_map/ppermute | solution.py:22
  34.1 36.4 %collective-permute-start.3 = (bf16[80,4736]{1,0:T(8,128)(2,1)}, bf16[80,4736]{1,0:T(8,128)(2,1)}, u32[]{:S(2)}, u32[]{:S(2)}) collective-permute-start(bf16[80,4736]{1,0:T(8,128)(2,1)} %slice.129), channel_id=1, source_target_pairs={{0,2},{1,3},{2,0},{3,1},{4,6},{5,7},{6,4},{7,5},{8,10},{9,11},{10,... | collective-permute-start | bytes 2273288 | tf_op jit(solution)/shard_map/ppermute | solution.py:22
  39.3 31.0 %collective-permute-start.5 = (bf16[80,2432]{1,0:T(8,128)(2,1)}, bf16[80,2432]{1,0:T(8,128)(2,1)}, u32[]{:S(2)}, u32[]{:S(2)}) collective-permute-start(bf16[80,2432]{1,0:T(8,128)(2,1)} %slice.132), channel_id=1, source_target_pairs={{0,2},{1,3},{2,0},{3,1},{4,6},{5,7},{6,4},{7,5},{8,10},{9,11},{10,... | collective-permute-start | bytes 1167368 | tf_op jit(solution)/shard_map/ppermute | solution.py:22
  78.6 76.8 %collective-permute-start.37 = (bf16[128,2432]{1,0:T(8,128)(2,1)S(1)}, bf16[128,2432]{1,0:T(8,128)(2,1)S(1)}, u32[]{:S(2)}, u32[]{:S(2)}) collective-permute-start(bf16[128,2432]{1,0:T(8,128)(2,1)S(1)} %fusion.25), channel_id=1, source_target_pairs={{4,20},{8,24},{12,28},{20,36},{24,40},{28,44},{36,52},{40,56},{44,... | collective-permute-start | bytes 1867784 | tf_op jit(solution)/shard_map/ppermute | solution.py:28
  87.6 65.7 %collective-permute-start.34 = (bf16[128,2432]{1,0:T(8,128)(2,1)S(1)}, bf16[128,2432]{1,0:T(8,128)(2,1)S(1)}, u32[]{:S(2)}, u32[]{:S(2)}) collective-permute-start(bf16[128,2432]{1,0:T(8,128)(2,1)S(1)} %fusion.30), channel_id=1, source_target_pairs={{4,20},{8,24},{12,28},{20,36},{24,40},{28,44},{36,52},{40,56},{44,... | collective-permute-start | bytes 1867784 | tf_op jit(solution)/shard_map/ppermute | solution.py:28
  97.7 41.0 %collective-permute-start.19 = (bf16[2304,128]{1,0:T(8,128)(2,1)S(1)}, bf16[2304,128]{1,0:T(8,128)(2,1)S(1)}, u32[]{:S(2)}, u32[]{:S(2)}) collective-permute-start(bf16[2304,128]{1,0:T(8,128)(2,1)S(1)} %fusion.22), channel_id=1, source_target_pairs={{4,20},{8,24},{12,28},{20,36},{24,40},{28,44},{36,52},{40,56},{44,... | collective-permute-start | bytes 1769480 | tf_op jit(solution)/shard_map/ppermute | solution.py:28
  103.5 47.8 %collective-permute-start.28 = (bf16[2304,128]{1,0:T(8,128)(2,1)S(1)}, bf16[2304,128]{1,0:T(8,128)(2,1)S(1)}, u32[]{:S(2)}, u32[]{:S(2)}) collective-permute-start(bf16[2304,128]{1,0:T(8,128)(2,1)S(1)} %fusion.23), channel_id=1, source_target_pairs={{4,20},{8,24},{12,28},{20,36},{24,40},{28,44},{36,52},{40,56},{44,... | collective-permute-start | bytes 1769480 | tf_op jit(solution)/shard_map/ppermute | solution.py:28
  112.7 52.0 %collective-permute-start.7 = (bf16[2432,128]{1,0:T(8,128)(2,1)S(1)}, bf16[2432,128]{1,0:T(8,128)(2,1)S(1)}, u32[]{:S(2)}, u32[]{:S(2)}) collective-permute-start(bf16[2432,128]{1,0:T(8,128)(2,1)S(1)} %fusion.26), channel_id=1, source_target_pairs={{4,20},{8,24},{12,28},{20,36},{24,40},{28,44},{36,52},{40,56},{44,... | collective-permute-start | bytes 1867784 | tf_op jit(solution)/shard_map/ppermute | solution.py:28
  138.7 39.3 %collective-permute-start.16 = (bf16[2432,128]{1,0:T(8,128)(2,1)S(1)}, bf16[2432,128]{1,0:T(8,128)(2,1)S(1)}, u32[]{:S(2)}, u32[]{:S(2)}) collective-permute-start(bf16[2432,128]{1,0:T(8,128)(2,1)S(1)} %fusion.27), channel_id=1, source_target_pairs={{4,20},{8,24},{12,28},{20,36},{24,40},{28,44},{36,52},{40,56},{44,... | collective-permute-start | bytes 1867784 | tf_op jit(solution)/shard_map/ppermute | solution.py:28
  151.3 40.0 %collective-permute-start.22 = (bf16[2432,128]{1,0:T(8,128)(2,1)S(1)}, bf16[2432,128]{1,0:T(8,128)(2,1)S(1)}, u32[]{:S(2)}, u32[]{:S(2)}) collective-permute-start(bf16[2432,128]{1,0:T(8,128)(2,1)S(1)} %fusion.28), channel_id=1, source_target_pairs={{4,20},{8,24},{12,28},{20,36},{24,40},{28,44},{36,52},{40,56},{44,... | collective-permute-start | bytes 1867784 | tf_op jit(solution)/shard_map/ppermute | solution.py:28
  153.3 50.8 %collective-permute-start.25 = (bf16[2432,128]{1,0:T(8,128)(2,1)S(1)}, bf16[2432,128]{1,0:T(8,128)(2,1)S(1)}, u32[]{:S(2)}, u32[]{:S(2)}) collective-permute-start(bf16[2432,128]{1,0:T(8,128)(2,1)S(1)} %fusion.29), channel_id=1, source_target_pairs={{4,20},{8,24},{12,28},{20,36},{24,40},{28,44},{36,52},{40,56},{44,... | collective-permute-start | bytes 1867784 | tf_op jit(solution)/shard_map/ppermute | solution.py:28
  155.3 50.3 %collective-permute-start.32 = (bf16[128,2304]{1,0:T(8,128)(2,1)S(1)}, bf16[128,2304]{1,0:T(8,128)(2,1)S(1)}, u32[]{:S(2)}, u32[]{:S(2)}) collective-permute-start(bf16[128,2304]{1,0:T(8,128)(2,1)S(1)} %broadcast_select_fusion.6), channel_id=1, source_target_pairs={{0,12},{4,8},{8,4},{12,0},{16,28},{20,24},{24,20},{28,16},{32,44},... | collective-permute-start | bytes 1769480 | tf_op jit(solution)/shard_map/ppermute | solution.py:28
  164.6 41.9 %collective-permute-start.20 = (bf16[2304,128]{1,0:T(8,128)(2,1)S(1)}, bf16[2304,128]{1,0:T(8,128)(2,1)S(1)}, u32[]{:S(2)}, u32[]{:S(2)}) collective-permute-start(bf16[2304,128]{1,0:T(8,128)(2,1)S(1)} %broadcast_select_fusion.8), channel_id=1, source_target_pairs={{0,12},{4,8},{8,4},{12,0},{16,28},{20,24},{24,20},{28,16},{32,44},... | collective-permute-start | bytes 1769480 | tf_op jit(solution)/shard_map/ppermute | solution.py:28
  178.0 30.5 %collective-permute-start.29 = (bf16[2304,128]{1,0:T(8,128)(2,1)S(1)}, bf16[2304,128]{1,0:T(8,128)(2,1)S(1)}, u32[]{:S(2)}, u32[]{:S(2)}) collective-permute-start(bf16[2304,128]{1,0:T(8,128)(2,1)S(1)} %broadcast_select_fusion.7), channel_id=1, source_target_pairs={{0,12},{4,8},{8,4},{12,0},{16,28},{20,24},{24,20},{28,16},{32,44},... | collective-permute-start | bytes 1769480 | tf_op jit(solution)/shard_map/ppermute | solution.py:28
  205.7 31.2 %collective-permute-start.8 = (bf16[2432,128]{1,0:T(8,128)(2,1)S(1)}, bf16[2432,128]{1,0:T(8,128)(2,1)S(1)}, u32[]{:S(2)}, u32[]{:S(2)}) collective-permute-start(bf16[2432,128]{1,0:T(8,128)(2,1)S(1)} %broadcast_select_fusion.5), channel_id=1, source_target_pairs={{0,12},{4,8},{8,4},{12,0},{16,28},{20,24},{24,20},{28,16},{32,44},... | collective-permute-start | bytes 1867784 | tf_op jit(solution)/shard_map/ppermute | solution.py:28
  206.6 43.6 %collective-permute-start.17 = (bf16[2432,128]{1,0:T(8,128)(2,1)S(1)}, bf16[2432,128]{1,0:T(8,128)(2,1)S(1)}, u32[]{:S(2)}, u32[]{:S(2)}) collective-permute-start(bf16[2432,128]{1,0:T(8,128)(2,1)S(1)} %broadcast_select_fusion.4), channel_id=1, source_target_pairs={{0,12},{4,8},{8,4},{12,0},{16,28},{20,24},{24,20},{28,16},{32,44},... | collective-permute-start | bytes 1867784 | tf_op jit(solution)/shard_map/ppermute | solution.py:28
  208.5 55.1 %collective-permute-start.23 = (bf16[2432,128]{1,0:T(8,128)(2,1)S(1)}, bf16[2432,128]{1,0:T(8,128)(2,1)S(1)}, u32[]{:S(2)}, u32[]{:S(2)}) collective-permute-start(bf16[2432,128]{1,0:T(8,128)(2,1)S(1)} %broadcast_select_fusion.3), channel_id=1, source_target_pairs={{0,12},{4,8},{8,4},{12,0},{16,28},{20,24},{24,20},{28,16},{32,44},... | collective-permute-start | bytes 1867784 | tf_op jit(solution)/shard_map/ppermute | solution.py:28
  210.2 64.7 %collective-permute-start.26 = (bf16[2432,128]{1,0:T(8,128)(2,1)S(1)}, bf16[2432,128]{1,0:T(8,128)(2,1)S(1)}, u32[]{:S(2)}, u32[]{:S(2)}) collective-permute-start(bf16[2432,128]{1,0:T(8,128)(2,1)S(1)} %broadcast_select_fusion.2), channel_id=1, source_target_pairs={{0,12},{4,8},{8,4},{12,0},{16,28},{20,24},{24,20},{28,16},{32,44},... | collective-permute-start | bytes 1867784 | tf_op jit(solution)/shard_map/ppermute | solution.py:28
  223.5 53.3 %collective-permute-start.33 = (bf16[128,2304]{1,0:T(8,128)(2,1)S(1)}, bf16[128,2304]{1,0:T(8,128)(2,1)S(1)}, u32[]{:S(2)}, u32[]{:S(2)}) collective-permute-start(bf16[128,2304]{1,0:T(8,128)(2,1)S(1)} %fusion.111), channel_id=1, source_target_pairs={{0,4},{4,0},{8,12},{12,8},{16,20},{20,16},{24,28},{28,24},{32,36},... | collective-permute-start | bytes 1769480 | tf_op jit(solution)/shard_map/ppermute | solution.py:28
  236.9 40.8 %collective-permute-start.21 = (bf16[2304,128]{1,0:T(8,128)(2,1)S(1)}, bf16[2304,128]{1,0:T(8,128)(2,1)S(1)}, u32[]{:S(2)}, u32[]{:S(2)}) collective-permute-start(bf16[2304,128]{1,0:T(8,128)(2,1)S(1)} %fusion.99), channel_id=1, source_target_pairs={{0,4},{4,0},{8,12},{12,8},{16,20},{20,16},{24,28},{28,24},{32,36},... | collective-permute-start | bytes 1769480 | tf_op jit(solution)/shard_map/ppermute | solution.py:28
  277.7 40.8 %collective-permute-start.18 = (bf16[2432,128]{1,0:T(8,128)(2,1)S(1)}, bf16[2432,128]{1,0:T(8,128)(2,1)S(1)}, u32[]{:S(2)}, u32[]{:S(2)}) collective-permute-start(bf16[2432,128]{1,0:T(8,128)(2,1)S(1)} %fusion.68), channel_id=1, source_target_pairs={{0,4},{4,0},{8,12},{12,8},{16,20},{20,16},{24,28},{28,24},{32,36},... | collective-permute-start | bytes 1867784 | tf_op jit(solution)/shard_map/ppermute | solution.py:28
  279.6 52.2 %collective-permute-start.24 = (bf16[2432,128]{1,0:T(8,128)(2,1)S(1)}, bf16[2432,128]{1,0:T(8,128)(2,1)S(1)}, u32[]{:S(2)}, u32[]{:S(2)}) collective-permute-start(bf16[2432,128]{1,0:T(8,128)(2,1)S(1)} %fusion.74), channel_id=1, source_target_pairs={{0,4},{4,0},{8,12},{12,8},{16,20},{20,16},{24,28},{28,24},{32,36},... | collective-permute-start | bytes 1867784 | tf_op jit(solution)/shard_map/ppermute | solution.py:28
  280.5 61.9 %collective-permute-start.27 = (bf16[2432,128]{1,0:T(8,128)(2,1)S(1)}, bf16[2432,128]{1,0:T(8,128)(2,1)S(1)}, u32[]{:S(2)}, u32[]{:S(2)}) collective-permute-start(bf16[2432,128]{1,0:T(8,128)(2,1)S(1)} %fusion.80), channel_id=1, source_target_pairs={{0,4},{4,0},{8,12},{12,8},{16,20},{20,16},{24,28},{28,24},{32,36},... | collective-permute-start | bytes 1867784 | tf_op jit(solution)/shard_map/ppermute | solution.py:28
  (21 other events, 286.3 us)

commit v4 on v3

--- a/solution.py
+++ b/solution.py
@@ -8,7 +8,7 @@
 PIECES = 3
 ROW = 4
 DOWN_CUTS = (0, 18, 37, 56)
-GATHER_CUTS = (0, 37, 56)
+GATHER_CUTS = (0, 28, 56)
 GATE_CUTS = (0, 19, 38, 56)
 UP_CUTS = (0, 19, 38, 56)
 
@@ -93,7 +93,13 @@
     hidden = (gate_pre * sig * up_pre).astype(bf16)
 
     dy = [jnp.concatenate([d0[:, s], d1[:, s], d2[c], d3[c]], axis=0) for c, s in enumerate(halves)]
-    dy_spans = [dy[0][:, spans[0]], dy[0][:, spans[1]], dy[1]]
+    split = halves[0].stop
+    across = [dy[0][:, spans[1].start : split], dy[1][:, : spans[1].stop - split]]
+    dy_spans = [
+        dy[0][:, spans[0]],
+        jnp.concatenate(across, axis=1),
+        dy[1][:, spans[2].start - split :],
+    ]
     weight = mass[0]
     rows = (((0,), (0,)), ((), ()))
 

time: 346 us -> 340 us (0.983)
  matrix products: 16.9 us -> 9.9 us
    ppermute x7, waiting for transfers between devices: 26 us -> 0.02 us  [swapped(): return lax.ppermute(array, 'mp', [(i, i ^ mask) for i in range(count)])]
    ppermute x6, waiting for transfers between devices: 10.8 us -> 29.9 us  [everyone(): other = lax.ppermute(ring, 'blk', [(r, r ^ bit) for r in range(count)])]
    ppermute x27, waiting for transfers between devices: 191 us -> 200 us  [moved(): return lax.ppermute(array, 'blk', pairs)]
  transfers between devices with their start and end apart: 40 -> 40, of which waited for: 25 -> 23; matrix products, arithmetic and copies ran while one was open for 11% -> 8% of each run, Pallas kernels for 0% -> 0%
where the time goes in v4:
time: 340 us; the launch traced here: 338 us
  waiting for transfers between devices  229 us (67%)
  starting transfers between devices  71.6 us (21%)
  other arithmetic  18.5 us (5%)
  matrix products  9.9 us (3%)
  local copies, waits for them, and re-layouts  6.09 us (2%)
    ppermute x27, waiting for transfers between devices, moved(): return lax.ppermute(array, 'blk', pairs)  200 us
    ppermute x27, starting transfers between devices, moved(): return lax.ppermute(array, 'blk', pairs)  48.4 us
    ppermute x6, waiting for transfers between devices, everyone(): other = lax.ppermute(ring, 'blk', [(r, r ^ bit) for r in range(count)])  29.9 us
    ppermute x6, starting transfers between devices, everyone(): other = lax.ppermute(ring, 'blk', [(r, r ^ bit) for r in range(count)])  15.7 us
    ppermute x7, starting transfers between devices, swapped(): return lax.ppermute(array, 'mp', [(i, i ^ mask) for i in range(count)])  7.44 us
    dot_general x9, matrix products, numer(): lax.dot_general(lhs, rhs, rows, preferred_element_type=f32) * scale_by  6.95 us
  transfers between devices with their start and end apart: 40, of which 23 were waited for; matrix products, arithmetic and copies ran while one was open for 8% of the time, Pallas kernels for 0%

profile of v4, /device:TPU:2, one launch (start us, length us, event | category | flops | bytes accessed | tf_op | source)
XLA Modules:
  0.0 338.0 jit_solution(3789289798671527871)
XLA Ops:
  0.7 3.3 pad_maximum_fusion.1
  21.7 3.3 collective-permute-start.13
  26.5 6.8 %collective-permute-start.14 = (f32[64]{0:T(128)S(1)}, f32[64]{0:T(128)S(1)}, u32[]{:S(2)}, u32[]{:S(2)}) collective-permute-start(f32[64]{0:T(128)S(1)} %add.150), channel_id=1, source_target_pairs={{0,64},{4,68},{8,72},{12,76},{16,80},{20,84},{24,88},{28,92},{32,9... | collective-permute-start | bytes 776 | tf_op jit(solution)/shard_map/ppermute | solution.py:36
  35.6 22.5 %collective-permute-done.15 = f32[64]{0:T(128)S(1)} collective-permute-done((f32[64]{0:T(128)S(1)}, f32[64]{0:T(128)S(1)}, u32[]{:S(2)}, u32[]{:S(2)}) %collective-permute-start.15) | collective-permute-done | bytes 288 | tf_op jit(solution)/shard_map/ppermute | solution.py:36
  69.3 3.8 %collective-permute-start.37 = (bf16[128,2432]{1,0:T(8,128)(2,1)S(1)}, bf16[128,2432]{1,0:T(8,128)(2,1)S(1)}, u32[]{:S(2)}, u32[]{:S(2)}) collective-permute-start(bf16[128,2432]{1,0:T(8,128)(2,1)S(1)} %fusion.25), channel_id=1, source_target_pairs={{4,20},{8,24},{12,28},{20,36},{24,40},{28,44},{36,52},{40,56},{44,... | collective-permute-start | bytes 1867784 | tf_op jit(solution)/shard_map/ppermute | solution.py:28
  79.3 3.8 %collective-permute-start.34 = (bf16[128,2432]{1,0:T(8,128)(2,1)S(1)}, bf16[128,2432]{1,0:T(8,128)(2,1)S(1)}, u32[]{:S(2)}, u32[]{:S(2)}) collective-permute-start(bf16[128,2432]{1,0:T(8,128)(2,1)S(1)} %fusion.30), channel_id=1, source_target_pairs={{4,20},{8,24},{12,28},{20,36},{24,40},{28,44},{36,52},{40,56},{44,... | collective-permute-start | bytes 1867784 | tf_op jit(solution)/shard_map/ppermute | solution.py:28
  84.7 5.0 %collective-permute-start.19 = (bf16[2304,128]{1,0:T(8,128)(2,1)S(1)}, bf16[2304,128]{1,0:T(8,128)(2,1)S(1)}, u32[]{:S(2)}, u32[]{:S(2)}) collective-permute-start(bf16[2304,128]{1,0:T(8,128)(2,1)S(1)} %fusion.22), channel_id=1, source_target_pairs={{4,20},{8,24},{12,28},{20,36},{24,40},{28,44},{36,52},{40,56},{44,... | collective-permute-start | bytes 1769480 | tf_op jit(solution)/shard_map/ppermute | solution.py:28
  96.7 8.7 %collective-permute-done.31 = bf16[128,2304]{1,0:T(8,128)(2,1)S(1)} collective-permute-done((bf16[128,2304]{1,0:T(8,128)(2,1)S(1)}, bf16[128,2304]{1,0:T(8,128)(2,1)S(1)}, u32[]{:S(2)}, u32[]{:S(2)}) %collective-permute-start.31) | collective-permute-done | bytes 589856 | tf_op jit(solution)/shard_map/ppermute | solution.py:28
  107.4 24.0 %collective-permute-done.19 = bf16[2304,128]{1,0:T(8,128)(2,1)S(1)} collective-permute-done((bf16[2304,128]{1,0:T(8,128)(2,1)S(1)}, bf16[2304,128]{1,0:T(8,128)(2,1)S(1)}, u32[]{:S(2)}, u32[]{:S(2)}) %collective-permute-start.19) | collective-permute-done | bytes 589856 | tf_op jit(solution)/shard_map/ppermute | solution.py:28
  133.4 10.7 %collective-permute-done.28 = bf16[2304,128]{1,0:T(8,128)(2,1)S(1)} collective-permute-done((bf16[2304,128]{1,0:T(8,128)(2,1)S(1)}, bf16[2304,128]{1,0:T(8,128)(2,1)S(1)}, u32[]{:S(2)}, u32[]{:S(2)}) %collective-permute-start.28) | collective-permute-done | bytes 589856 | tf_op jit(solution)/shard_map/ppermute | solution.py:28
  149.7 7.7 %collective-permute-done.7 = bf16[2432,128]{1,0:T(8,128)(2,1)S(1)} collective-permute-done((bf16[2432,128]{1,0:T(8,128)(2,1)S(1)}, bf16[2432,128]{1,0:T(8,128)(2,1)S(1)}, u32[]{:S(2)}, u32[]{:S(2)}) %collective-permute-start.7) | collective-permute-done | bytes 622624 | tf_op jit(solution)/shard_map/ppermute | solution.py:28
  158.9 11.8 %collective-permute-done.16 = bf16[2432,128]{1,0:T(8,128)(2,1)S(1)} collective-permute-done((bf16[2432,128]{1,0:T(8,128)(2,1)S(1)}, bf16[2432,128]{1,0:T(8,128)(2,1)S(1)}, u32[]{:S(2)}, u32[]{:S(2)}) %collective-permute-start.16) | collective-permute-done | bytes 622624 | tf_op jit(solution)/shard_map/ppermute | solution.py:28
  172.3 11.8 %collective-permute-done.22 = bf16[2432,128]{1,0:T(8,128)(2,1)S(1)} collective-permute-done((bf16[2432,128]{1,0:T(8,128)(2,1)S(1)}, bf16[2432,128]{1,0:T(8,128)(2,1)S(1)}, u32[]{:S(2)}, u32[]{:S(2)}) %collective-permute-start.22) | collective-permute-done | bytes 622624 | tf_op jit(solution)/shard_map/ppermute | solution.py:28
  185.6 11.5 %collective-permute-done.25 = bf16[2432,128]{1,0:T(8,128)(2,1)S(1)} collective-permute-done((bf16[2432,128]{1,0:T(8,128)(2,1)S(1)}, bf16[2432,128]{1,0:T(8,128)(2,1)S(1)}, u32[]{:S(2)}, u32[]{:S(2)}) %collective-permute-start.25) | collective-permute-done | bytes 622624 | tf_op jit(solution)/shard_map/ppermute | solution.py:28
  204.8 11.5 %collective-permute-done.35 = bf16[128,2432]{1,0:T(8,128)(2,1)S(1)} collective-permute-done((bf16[128,2432]{1,0:T(8,128)(2,1)S(1)}, bf16[128,2432]{1,0:T(8,128)(2,1)S(1)}, u32[]{:S(2)}, u32[]{:S(2)}) %collective-permute-start.35) | collective-permute-done | bytes 622624 | tf_op jit(solution)/shard_map/ppermute | solution.py:28
  217.9 11.7 %collective-permute-done.8 = bf16[2432,128]{1,0:T(8,128)(2,1)S(1)} collective-permute-done((bf16[2432,128]{1,0:T(8,128)(2,1)S(1)}, bf16[2432,128]{1,0:T(8,128)(2,1)S(1)}, u32[]{:S(2)}, u32[]{:S(2)}) %collective-permute-start.8) | collective-permute-done | bytes 622624 | tf_op jit(solution)/shard_map/ppermute | solution.py:28
  231.3 11.7 %collective-permute-done.17 = bf16[2432,128]{1,0:T(8,128)(2,1)S(1)} collective-permute-done((bf16[2432,128]{1,0:T(8,128)(2,1)S(1)}, bf16[2432,128]{1,0:T(8,128)(2,1)S(1)}, u32[]{:S(2)}, u32[]{:S(2)}) %collective-permute-start.17) | collective-permute-done | bytes 622624 | tf_op jit(solution)/shard_map/ppermute | solution.py:28
  244.6 11.7 %collective-permute-done.23 = bf16[2432,128]{1,0:T(8,128)(2,1)S(1)} collective-permute-done((bf16[2432,128]{1,0:T(8,128)(2,1)S(1)}, bf16[2432,128]{1,0:T(8,128)(2,1)S(1)}, u32[]{:S(2)}, u32[]{:S(2)}) %collective-permute-start.23) | collective-permute-done | bytes 622624 | tf_op jit(solution)/shard_map/ppermute | solution.py:28
  257.9 10.3 %collective-permute-done.26 = bf16[2432,128]{1,0:T(8,128)(2,1)S(1)} collective-permute-done((bf16[2432,128]{1,0:T(8,128)(2,1)S(1)}, bf16[2432,128]{1,0:T(8,128)(2,1)S(1)}, u32[]{:S(2)}, u32[]{:S(2)}) %collective-permute-start.26) | collective-permute-done | bytes 622624 | tf_op jit(solution)/shard_map/ppermute | solution.py:28
  275.8 9.3 %collective-permute-done.36 = bf16[128,2432]{1,0:T(8,128)(2,1)S(1)} collective-permute-done((bf16[128,2432]{1,0:T(8,128)(2,1)S(1)}, bf16[128,2432]{1,0:T(8,128)(2,1)S(1)}, u32[]{:S(2)}, u32[]{:S(2)}) %collective-permute-start.36) | collective-permute-done | bytes 622624 | tf_op jit(solution)/shard_map/ppermute | solution.py:28
  286.9 11.6 %collective-permute-done.9 = bf16[2432,128]{1,0:T(8,128)(2,1)S(1)} collective-permute-done((bf16[2432,128]{1,0:T(8,128)(2,1)S(1)}, bf16[2432,128]{1,0:T(8,128)(2,1)S(1)}, u32[]{:S(2)}, u32[]{:S(2)}) %collective-permute-start.9) | collective-permute-done | bytes 622624 | tf_op jit(solution)/shard_map/ppermute | solution.py:28
  298.8 13.0 %collective-permute-done.18 = bf16[2432,128]{1,0:T(8,128)(2,1)S(1)} collective-permute-done((bf16[2432,128]{1,0:T(8,128)(2,1)S(1)}, bf16[2432,128]{1,0:T(8,128)(2,1)S(1)}, u32[]{:S(2)}, u32[]{:S(2)}) %collective-permute-start.18) | collective-permute-done | bytes 622624 | tf_op jit(solution)/shard_map/ppermute | solution.py:28
  313.5 11.7 %collective-permute-done.24 = bf16[2432,128]{1,0:T(8,128)(2,1)S(1)} collective-permute-done((bf16[2432,128]{1,0:T(8,128)(2,1)S(1)}, bf16[2432,128]{1,0:T(8,128)(2,1)S(1)}, u32[]{:S(2)}, u32[]{:S(2)}) %collective-permute-start.24) | collective-permute-done | bytes 622624 | tf_op jit(solution)/shard_map/ppermute | solution.py:28
  325.5 10.8 %collective-permute-done.27 = bf16[2432,128]{1,0:T(8,128)(2,1)S(1)} collective-permute-done((bf16[2432,128]{1,0:T(8,128)(2,1)S(1)}, bf16[2432,128]{1,0:T(8,128)(2,1)S(1)}, u32[]{:S(2)}, u32[]{:S(2)}) %collective-permute-start.27) | collective-permute-done | bytes 622624 | tf_op jit(solution)/shard_map/ppermute | solution.py:28
  (129 shorter events, 87.7 us)
Async XLA Ops:
  4.0 58.2 %collective-permute-start = (bf16[160,7168]{1,0:T(8,128)(2,1)}, bf16[160,7168]{1,0:T(8,128)(2,1)}, u32[]{:S(2)}, u32[]{:S(2)}) collective-permute-start(bf16[160,7168]{1,0:T(8,128)(2,1)} %pad_maximum_fusion.1), channel_id=1, source_target_pairs={{0,1},{1,0},{2,3},{3,2},{4,5},{5,4},{6,7},{7,6},{8,9},{9,8},{10,11... | collective-permute-start | bytes 6881288 | tf_op jit(solution)/shard_map/ppermute | solution.py:22
  4.0 54.8 %collective-permute-start.1 = (bf16[80,7168]{1,0:T(8,128)(2,1)S(1)}, bf16[80,7168]{1,0:T(8,128)(2,1)S(1)}, u32[]{:S(2)}, u32[]{:S(2)}) collective-permute-start(bf16[80,7168]{1,0:T(8,128)(2,1)S(1)} %bitcast.60), channel_id=1, source_target_pairs={{0,2},{1,3},{2,0},{3,1},{4,6},{5,7},{6,4},{7,5},{8,10},{9,11},{10,... | collective-permute-start | bytes 3440648 | tf_op jit(solution)/shard_map/ppermute | solution.py:22
  9.5 51.9 %collective-permute-start.3 = (bf16[80,3584]{1,0:T(8,128)(2,1)}, bf16[80,3584]{1,0:T(8,128)(2,1)S(1)}, u32[]{:S(2)}, u32[]{:S(2)}) collective-permute-start(bf16[80,3584]{1,0:T(8,128)(2,1)} %get-tuple-element.13), channel_id=1, source_target_pairs={{0,2},{1,3},{2,0},{3,1},{4,6},{5,7},{6,4},{7,5},{8,10},{9,11},{10,... | collective-permute-start | bytes 1720328 | tf_op jit(solution)/shard_map/ppermute | solution.py:22
  11.6 50.5 %collective-permute-start.5 = (bf16[80,3584]{1,0:T(8,128)(2,1)}, bf16[80,3584]{1,0:T(8,128)(2,1)S(1)}, u32[]{:S(2)}, u32[]{:S(2)}) collective-permute-start(bf16[80,3584]{1,0:T(8,128)(2,1)} %get-tuple-element.14), channel_id=1, source_target_pairs={{0,2},{1,3},{2,0},{3,1},{4,6},{5,7},{6,4},{7,5},{8,10},{9,11},{10,... | collective-permute-start | bytes 1720328 | tf_op jit(solution)/shard_map/ppermute | solution.py:22
  69.3 76.7 %collective-permute-start.37 = (bf16[128,2432]{1,0:T(8,128)(2,1)S(1)}, bf16[128,2432]{1,0:T(8,128)(2,1)S(1)}, u32[]{:S(2)}, u32[]{:S(2)}) collective-permute-start(bf16[128,2432]{1,0:T(8,128)(2,1)S(1)} %fusion.25), channel_id=1, source_target_pairs={{4,20},{8,24},{12,28},{20,36},{24,40},{28,44},{36,52},{40,56},{44,... | collective-permute-start | bytes 1867784 | tf_op jit(solution)/shard_map/ppermute | solution.py:28
  79.3 68.8 %collective-permute-start.34 = (bf16[128,2432]{1,0:T(8,128)(2,1)S(1)}, bf16[128,2432]{1,0:T(8,128)(2,1)S(1)}, u32[]{:S(2)}, u32[]{:S(2)}) collective-permute-start(bf16[128,2432]{1,0:T(8,128)(2,1)S(1)} %fusion.30), channel_id=1, source_target_pairs={{4,20},{8,24},{12,28},{20,36},{24,40},{28,44},{36,52},{40,56},{44,... | collective-permute-start | bytes 1867784 | tf_op jit(solution)/shard_map/ppermute | solution.py:28
  84.7 46.7 %collective-permute-start.19 = (bf16[2304,128]{1,0:T(8,128)(2,1)S(1)}, bf16[2304,128]{1,0:T(8,128)(2,1)S(1)}, u32[]{:S(2)}, u32[]{:S(2)}) collective-permute-start(bf16[2304,128]{1,0:T(8,128)(2,1)S(1)} %fusion.22), channel_id=1, source_target_pairs={{4,20},{8,24},{12,28},{20,36},{24,40},{28,44},{36,52},{40,56},{44,... | collective-permute-start | bytes 1769480 | tf_op jit(solution)/shard_map/ppermute | solution.py:28
  90.5 53.6 %collective-permute-start.28 = (bf16[2304,128]{1,0:T(8,128)(2,1)S(1)}, bf16[2304,128]{1,0:T(8,128)(2,1)S(1)}, u32[]{:S(2)}, u32[]{:S(2)}) collective-permute-start(bf16[2304,128]{1,0:T(8,128)(2,1)S(1)} %fusion.23), channel_id=1, source_target_pairs={{4,20},{8,24},{12,28},{20,36},{24,40},{28,44},{36,52},{40,56},{44,... | collective-permute-start | bytes 1769480 | tf_op jit(solution)/shard_map/ppermute | solution.py:28
  105.4 52.0 %collective-permute-start.7 = (bf16[2432,128]{1,0:T(8,128)(2,1)S(1)}, bf16[2432,128]{1,0:T(8,128)(2,1)S(1)}, u32[]{:S(2)}, u32[]{:S(2)}) collective-permute-start(bf16[2432,128]{1,0:T(8,128)(2,1)S(1)} %fusion.26), channel_id=1, source_target_pairs={{4,20},{8,24},{12,28},{20,36},{24,40},{28,44},{36,52},{40,56},{44,... | collective-permute-start | bytes 1867784 | tf_op jit(solution)/shard_map/ppermute | solution.py:28
  131.4 39.3 %collective-permute-start.16 = (bf16[2432,128]{1,0:T(8,128)(2,1)S(1)}, bf16[2432,128]{1,0:T(8,128)(2,1)S(1)}, u32[]{:S(2)}, u32[]{:S(2)}) collective-permute-start(bf16[2432,128]{1,0:T(8,128)(2,1)S(1)} %fusion.27), channel_id=1, source_target_pairs={{4,20},{8,24},{12,28},{20,36},{24,40},{28,44},{36,52},{40,56},{44,... | collective-permute-start | bytes 1867784 | tf_op jit(solution)/shard_map/ppermute | solution.py:28
  144.0 40.0 %collective-permute-start.22 = (bf16[2432,128]{1,0:T(8,128)(2,1)S(1)}, bf16[2432,128]{1,0:T(8,128)(2,1)S(1)}, u32[]{:S(2)}, u32[]{:S(2)}) collective-permute-start(bf16[2432,128]{1,0:T(8,128)(2,1)S(1)} %fusion.28), channel_id=1, source_target_pairs={{4,20},{8,24},{12,28},{20,36},{24,40},{28,44},{36,52},{40,56},{44,... | collective-permute-start | bytes 1867784 | tf_op jit(solution)/shard_map/ppermute | solution.py:28
  146.0 51.1 %collective-permute-start.25 = (bf16[2432,128]{1,0:T(8,128)(2,1)S(1)}, bf16[2432,128]{1,0:T(8,128)(2,1)S(1)}, u32[]{:S(2)}, u32[]{:S(2)}) collective-permute-start(bf16[2432,128]{1,0:T(8,128)(2,1)S(1)} %fusion.29), channel_id=1, source_target_pairs={{4,20},{8,24},{12,28},{20,36},{24,40},{28,44},{36,52},{40,56},{44,... | collective-permute-start | bytes 1867784 | tf_op jit(solution)/shard_map/ppermute | solution.py:28
  148.0 50.6 %collective-permute-start.32 = (bf16[128,2304]{1,0:T(8,128)(2,1)S(1)}, bf16[128,2304]{1,0:T(8,128)(2,1)S(1)}, u32[]{:S(2)}, u32[]{:S(2)}) collective-permute-start(bf16[128,2304]{1,0:T(8,128)(2,1)S(1)} %broadcast_select_fusion.6), channel_id=1, source_target_pairs={{0,12},{4,8},{8,4},{12,0},{16,28},{20,24},{24,20},{28,16},{32,44},... | collective-permute-start | bytes 1769480 | tf_op jit(solution)/shard_map/ppermute | solution.py:28
  157.4 42.2 %collective-permute-start.20 = (bf16[2304,128]{1,0:T(8,128)(2,1)S(1)}, bf16[2304,128]{1,0:T(8,128)(2,1)S(1)}, u32[]{:S(2)}, u32[]{:S(2)}) collective-permute-start(bf16[2304,128]{1,0:T(8,128)(2,1)S(1)} %broadcast_select_fusion.8), channel_id=1, source_target_pairs={{0,12},{4,8},{8,4},{12,0},{16,28},{20,24},{24,20},{28,16},{32,44},... | collective-permute-start | bytes 1769480 | tf_op jit(solution)/shard_map/ppermute | solution.py:28
  170.7 30.8 %collective-permute-start.29 = (bf16[2304,128]{1,0:T(8,128)(2,1)S(1)}, bf16[2304,128]{1,0:T(8,128)(2,1)S(1)}, u32[]{:S(2)}, u32[]{:S(2)}) collective-permute-start(bf16[2304,128]{1,0:T(8,128)(2,1)S(1)} %broadcast_select_fusion.7), channel_id=1, source_target_pairs={{0,12},{4,8},{8,4},{12,0},{16,28},{20,24},{24,20},{28,16},{32,44},... | collective-permute-start | bytes 1769480 | tf_op jit(solution)/shard_map/ppermute | solution.py:28
  198.7 31.0 %collective-permute-start.8 = (bf16[2432,128]{1,0:T(8,128)(2,1)S(1)}, bf16[2432,128]{1,0:T(8,128)(2,1)S(1)}, u32[]{:S(2)}, u32[]{:S(2)}) collective-permute-start(bf16[2432,128]{1,0:T(8,128)(2,1)S(1)} %broadcast_select_fusion.5), channel_id=1, source_target_pairs={{0,12},{4,8},{8,4},{12,0},{16,28},{20,24},{24,20},{28,16},{32,44},... | collective-permute-start | bytes 1867784 | tf_op jit(solution)/shard_map/ppermute | solution.py:28
  199.6 43.4 %collective-permute-start.17 = (bf16[2432,128]{1,0:T(8,128)(2,1)S(1)}, bf16[2432,128]{1,0:T(8,128)(2,1)S(1)}, u32[]{:S(2)}, u32[]{:S(2)}) collective-permute-start(bf16[2432,128]{1,0:T(8,128)(2,1)S(1)} %broadcast_select_fusion.4), channel_id=1, source_target_pairs={{0,12},{4,8},{8,4},{12,0},{16,28},{20,24},{24,20},{28,16},{32,44},... | collective-permute-start | bytes 1867784 | tf_op jit(solution)/shard_map/ppermute | solution.py:28
  201.5 54.8 %collective-permute-start.23 = (bf16[2432,128]{1,0:T(8,128)(2,1)S(1)}, bf16[2432,128]{1,0:T(8,128)(2,1)S(1)}, u32[]{:S(2)}, u32[]{:S(2)}) collective-permute-start(bf16[2432,128]{1,0:T(8,128)(2,1)S(1)} %broadcast_select_fusion.3), channel_id=1, source_target_pairs={{0,12},{4,8},{8,4},{12,0},{16,28},{20,24},{24,20},{28,16},{32,44},... | collective-permute-start | bytes 1867784 | tf_op jit(solution)/shard_map/ppermute | solution.py:28
  202.9 65.3 %collective-permute-start.26 = (bf16[2432,128]{1,0:T(8,128)(2,1)S(1)}, bf16[2432,128]{1,0:T(8,128)(2,1)S(1)}, u32[]{:S(2)}, u32[]{:S(2)}) collective-permute-start(bf16[2432,128]{1,0:T(8,128)(2,1)S(1)} %broadcast_select_fusion.2), channel_id=1, source_target_pairs={{0,12},{4,8},{8,4},{12,0},{16,28},{20,24},{24,20},{28,16},{32,44},... | collective-permute-start | bytes 1867784 | tf_op jit(solution)/shard_map/ppermute | solution.py:28
  216.3 53.8 %collective-permute-start.33 = (bf16[128,2304]{1,0:T(8,128)(2,1)S(1)}, bf16[128,2304]{1,0:T(8,128)(2,1)S(1)}, u32[]{:S(2)}, u32[]{:S(2)}) collective-permute-start(bf16[128,2304]{1,0:T(8,128)(2,1)S(1)} %fusion.94), channel_id=1, source_target_pairs={{0,4},{4,0},{8,12},{12,8},{16,20},{20,16},{24,28},{28,24},{32,36},... | collective-permute-start | bytes 1769480 | tf_op jit(solution)/shard_map/ppermute | solution.py:28
  229.6 41.4 %collective-permute-start.21 = (bf16[2304,128]{1,0:T(8,128)(2,1)S(1)}, bf16[2304,128]{1,0:T(8,128)(2,1)S(1)}, u32[]{:S(2)}, u32[]{:S(2)}) collective-permute-start(bf16[2304,128]{1,0:T(8,128)(2,1)S(1)} %fusion.82), channel_id=1, source_target_pairs={{0,4},{4,0},{8,12},{12,8},{16,20},{20,16},{24,28},{28,24},{32,36},... | collective-permute-start | bytes 1769480 | tf_op jit(solution)/shard_map/ppermute | solution.py:28
  271.0 40.8 %collective-permute-start.18 = (bf16[2432,128]{1,0:T(8,128)(2,1)S(1)}, bf16[2432,128]{1,0:T(8,128)(2,1)S(1)}, u32[]{:S(2)}, u32[]{:S(2)}) collective-permute-start(bf16[2432,128]{1,0:T(8,128)(2,1)S(1)} %fusion.52), channel_id=1, source_target_pairs={{0,4},{4,0},{8,12},{12,8},{16,20},{20,16},{24,28},{28,24},{32,36},... | collective-permute-start | bytes 1867784 | tf_op jit(solution)/shard_map/ppermute | solution.py:28
  272.9 52.2 %collective-permute-start.24 = (bf16[2432,128]{1,0:T(8,128)(2,1)S(1)}, bf16[2432,128]{1,0:T(8,128)(2,1)S(1)}, u32[]{:S(2)}, u32[]{:S(2)}) collective-permute-start(bf16[2432,128]{1,0:T(8,128)(2,1)S(1)} %fusion.58), channel_id=1, source_target_pairs={{0,4},{4,0},{8,12},{12,8},{16,20},{20,16},{24,28},{28,24},{32,36},... | collective-permute-start | bytes 1867784 | tf_op jit(solution)/shard_map/ppermute | solution.py:28
  273.8 62.5 %collective-permute-start.27 = (bf16[2432,128]{1,0:T(8,128)(2,1)S(1)}, bf16[2432,128]{1,0:T(8,128)(2,1)S(1)}, u32[]{:S(2)}, u32[]{:S(2)}) collective-permute-start(bf16[2432,128]{1,0:T(8,128)(2,1)S(1)} %fusion.64), channel_id=1, source_target_pairs={{0,4},{4,0},{8,12},{12,8},{16,20},{20,16},{24,28},{28,24},{32,36},... | collective-permute-start | bytes 1867784 | tf_op jit(solution)/shard_map/ppermute | solution.py:28
  (21 other events, 252.2 us)
